TPU v7x, 32 devices: a whole 2x2x4 slice. The times are simulated.
32 devices in a mesh: gx: 2 (over y), gy: 4 (over z), gz: 4 (over x, core).
Axes of the slice: x: 2, y: 2, z: 4, core: 2. Of those that a mesh axis runs over, the one named last changes fastest.
Arguments:
- conserved: float32 [5, 16, 32, 512], P(None, 'gx', 'gy', 'gz'), may hold values from -3 to 4, as said below
- sigma_guess: float32 [16, 32, 512], P('gx', 'gy', 'gz'), may hold values from -30 to 30
Outputs:
- advanced: float32 [5, 16, 32, 512], P(None, 'gx', 'gy', 'gz')
- sigma_field: float32 [16, 32, 512], P('gx', 'gy', 'gz')
Inputs may be any that keep to these rules, and one draw needn't show every extreme that they name: `conserved`: component 0 (density) lies between 0.5 and 2, components 1 to 3 (momenta) between -3 and 3, component 4 (energy) between 1 and 4.
All inputs are finite; a program needn't handle non-finite values.
Results may differ from a plain program's by a relative error of at most 0.00002.
Values sent between devices are 32-bit elements; how exact they have to be, the bound alone decides.
A program may use at most 64 MiB of HBM per device.

v0:
```python
import jax
import jax.numpy as jnp
from jax import lax
from jax.sharding import PartitionSpec as P

SWEEPS = 4


ALPHA = 10.0
GAMMA = 1.4
LAMBDA = 3.0
STEP_DT = 0.4


def extended(cells, sides, width):
    for axis, dim in sides:
        count = lax.axis_size(axis)
        head = lax.slice_in_dim(cells, 0, width, axis=dim)
        tail = lax.slice_in_dim(cells, cells.shape[dim] - width, cells.shape[dim], axis=dim)
        cells = jnp.concatenate(
            [
                lax.ppermute(tail, axis, [(i, (i + 1) % count) for i in range(count)]),
                cells,
                lax.ppermute(head, axis, [((i + 1) % count, i) for i in range(count)]),
            ],
            axis=dim,
        )
    return cells


def trim_margin(field, margin):
    return field[..., margin:-margin, margin:-margin, margin:-margin]


def central(field, direction):
    length = field.shape[direction]
    upper_part = lax.slice_in_dim(field, 2, length, axis=direction)
    lower_part = lax.slice_in_dim(field, 0, length - 2, axis=direction)
    slope = 0.5 * (upper_part - lower_part)
    for across in range(3):
        if across != direction:
            slope = lax.slice_in_dim(slope, 1, slope.shape[across] - 1, axis=across)
    return slope


def neighbour(field, direction, offset):
    length = field.shape[direction]
    moved = lax.slice_in_dim(field, 1 - offset, length - 1 - offset, axis=direction)
    for across in range(3):
        if across != direction:
            moved = lax.slice_in_dim(moved, 1, moved.shape[across] - 1, axis=across)
    return moved


def source_term(velocity):
    gradient = [[central(velocity[member], across) for across in range(3)] for member in range(3)]
    trace_sq = jnp.zeros_like(gradient[0][0])
    for member in range(3):
        for across in range(3):
            trace_sq = trace_sq + gradient[member][across] * gradient[across][member]
    divergence = gradient[0][0] + gradient[1][1] + gradient[2][2]
    return trace_sq + divergence * divergence


def jacobi_sweep(sigma_now, inv_density, source):
    centre = trim_margin(inv_density, 1)
    acc_num = jnp.zeros_like(centre)
    acc_den = jnp.zeros_like(centre)
    for direction in range(3):
        for offset in (1, -1):
            weight_face = 0.5 * (centre + neighbour(inv_density, direction, offset))
            acc_num = acc_num + weight_face * neighbour(sigma_now, direction, offset)
            acc_den = acc_den + weight_face
    return (ALPHA * source + ALPHA * acc_num) / (centre + ALPHA * acc_den)


def physical(states, sigma_face, direction):
    density = states[0]
    normal_speed = states[1 + direction] / density
    kinetic = (
        0.5 * (states[1] * states[1] + states[2] * states[2] + states[3] * states[3]) / density
    )
    pressure = (GAMMA - 1.0) * (states[4] - kinetic) + sigma_face
    flux_rows = [states[1 + direction]]
    for member in range(3):
        flux_term = states[1 + member] * normal_speed
        if member == direction:
            flux_term = flux_term + pressure
        flux_rows.append(flux_term)
    flux_rows.append((states[4] + pressure) * normal_speed)
    return jnp.stack(flux_rows)


def flux_change(padded_state, padded_sigma, direction):
    strip = padded_state
    sigma_strip = padded_sigma
    for across in range(3):
        if across != direction:
            strip = lax.slice_in_dim(strip, 2, strip.shape[across + 1] - 2, axis=across + 1)
            sigma_strip = lax.slice_in_dim(
                sigma_strip, 2, sigma_strip.shape[across] - 2, axis=across
            )
    span_len = sigma_strip.shape[direction] - 4

    def window(field, start, axis_at):
        return lax.slice_in_dim(field, start, start + span_len + 1, axis=axis_at)

    axis_q = direction + 1
    left_state = (
        5.0 * window(strip, 1, axis_q) + 2.0 * window(strip, 2, axis_q) - window(strip, 0, axis_q)
    ) / 6.0
    right_state = (
        2.0 * window(strip, 1, axis_q) + 5.0 * window(strip, 2, axis_q) - window(strip, 3, axis_q)
    ) / 6.0
    left_sigma = (
        5.0 * window(sigma_strip, 1, direction)
        + 2.0 * window(sigma_strip, 2, direction)
        - window(sigma_strip, 0, direction)
    ) / 6.0
    right_sigma = (
        2.0 * window(sigma_strip, 1, direction)
        + 5.0 * window(sigma_strip, 2, direction)
        - window(sigma_strip, 3, direction)
    ) / 6.0
    face_flux = 0.5 * (
        physical(left_state, left_sigma, direction) + physical(right_state, right_sigma, direction)
    ) - 0.5 * LAMBDA * (right_state - left_state)
    return lax.slice_in_dim(face_flux, 1, span_len + 1, axis=axis_q) - lax.slice_in_dim(
        face_flux, 0, span_len, axis=axis_q
    )


def on_device(conserved, sigma_guess):
    packed = jnp.concatenate([conserved, sigma_guess[None]], axis=0)
    near_rim = extended(packed, (("gx", 1), ("gy", 2), ("gz", 3)), 2)
    inner_rim = trim_margin(near_rim, 1)
    inv_density = 1.0 / inner_rim[0]
    velocity = inner_rim[1:4] / inner_rim[0]
    source = source_term(velocity)
    sigma_now = jacobi_sweep(inner_rim[5], inv_density, source)
    for sweep_no in range(SWEEPS - 1):
        bordered = extended(sigma_now, (("gx", 0), ("gy", 1), ("gz", 2)), 1)
        sigma_now = jacobi_sweep(bordered, inv_density, source)
    padded_sigma = extended(sigma_now, (("gx", 0), ("gy", 1), ("gz", 2)), 2)
    padded_state = near_rim[:5]
    tendency = jnp.zeros_like(conserved)
    for direction in range(3):
        tendency = tendency - flux_change(padded_state, padded_sigma, direction)
    advanced = conserved + STEP_DT * tendency
    return (advanced, sigma_now)


def solution(mesh):
    in_specs = (P(None, "gx", "gy", "gz"), P("gx", "gy", "gz"))
    out_specs = (P(None, "gx", "gy", "gz"), P("gx", "gy", "gz"))
    return jax.shard_map(
        on_device, mesh=mesh, in_specs=in_specs, out_specs=out_specs, check_vma=False
    )
```

profile of v0, /device:TPU:0, one launch (start us, length us, event | category | flops | bytes accessed | tf_op | source)
XLA Modules:
  0.0 90.3 jit_solution(9501687383495770173)
XLA Ops:
  1.5 3.1 %collective-permute-start.1 = (f32[6,2,8,128]{3,2,1,0:T(8,128)S(1)}, f32[6,2,8,128]{3,2,1,0:T(8,128)S(1)}, u32[]{:S(2)}, u32[]{:S(2)}) collective-permute-start(f32[6,2,8,128]{3,2,1,0:T(8,128)S(1)} %get-tuple-element.43), channel_id=1, source_target_pairs={{16,0},{0,16},{17,1},{1,17},{18,2},{2,18},{19,3},{3,19},{20,4},{4,... | collective-permute-start | bytes 147464 | tf_op jit(solution)/shard_map/ppermute | solution.py:24
  4.6 2.0 %collective-permute-done.1 = f32[6,2,8,128]{3,2,1,0:T(8,128)S(1)} collective-permute-done((f32[6,2,8,128]{3,2,1,0:T(8,128)S(1)}, f32[6,2,8,128]{3,2,1,0:T(8,128)S(1)}, u32[]{:S(2)}, u32[]{:S(2)}) %collective-permute-start.1) | collective-permute-done | bytes 49184 | tf_op jit(solution)/shard_map/ppermute | solution.py:24
  6.6 2.0 %collective-permute-done = f32[6,2,8,128]{3,2,1,0:T(8,128)S(1)} collective-permute-done((f32[6,2,8,128]{3,2,1,0:T(8,128)S(1)}, f32[6,2,8,128]{3,2,1,0:T(8,128)S(1)}, u32[]{:S(2)}, u32[]{:S(2)}) %collective-permute-start) | collective-permute-done | bytes 49184 | tf_op jit(solution)/shard_map/ppermute | solution.py:22
  9.7 3.7 %collective-permute-start.3 = (f32[6,12,2,128]{3,2,1,0:T(2,128)S(1)}, f32[6,12,2,128]{3,2,1,0:T(2,128)S(1)}, u32[]{:S(2)}, u32[]{:S(2)}) collective-permute-start(f32[6,12,2,128]{3,2,1,0:T(2,128)S(1)} %get-tuple-element.37), channel_id=1, source_target_pairs={{4,0},{8,4},{12,8},{0,12},{5,1},{9,5},{13,9},{1,13},{6,2},{10,6},{... | collective-permute-start | bytes 221192 | tf_op jit(solution)/shard_map/ppermute | solution.py:24
  15.3 4.2 %collective-permute-done.2 = f32[6,12,2,128]{3,2,1,0:T(2,128)S(1)} collective-permute-done((f32[6,12,2,128]{3,2,1,0:T(2,128)S(1)}, f32[6,12,2,128]{3,2,1,0:T(2,128)S(1)}, u32[]{:S(2)}, u32[]{:S(2)}) %collective-permute-start.2) | collective-permute-done | bytes 73760 | tf_op jit(solution)/shard_map/ppermute | solution.py:22
  23.0 2.7 %collective-permute-done.4 = f32[6,12,12,2]{2,3,1,0:T(2,128)} collective-permute-done((f32[6,12,12,2]{2,3,1,0:T(2,128)}, f32[6,12,12,2]{2,3,1,0:T(2,128)}, u32[]{:S(2)}, u32[]{:S(2)}) %collective-permute-start.4) | collective-permute-done | bytes 6944 | tf_op jit(solution)/shard_map/ppermute | solution.py:22
  29.8 1.5 %collective-permute-start.6 = (f32[1,8,128]{2,1,0:T(8,128)S(1)}, f32[1,8,128]{2,1,0:T(8,128)S(1)}, u32[]{:S(2)}, u32[]{:S(2)}) collective-permute-start(f32[1,8,128]{2,1,0:T(8,128)S(1)} %get-tuple-element.80), channel_id=1, source_target_pairs={{0,16},{16,0},{1,17},{17,1},{2,18},{18,2},{3,19},{19,3},{4,20},{20... | collective-permute-start | bytes 12296 | tf_op jit(solution)/shard_map/ppermute | solution.py:22
  31.3 1.6 %collective-permute-done.7 = f32[1,8,128]{2,1,0:T(8,128)S(1)} collective-permute-done((f32[1,8,128]{2,1,0:T(8,128)S(1)}, f32[1,8,128]{2,1,0:T(8,128)S(1)}, u32[]{:S(2)}, u32[]{:S(2)}) %collective-permute-start.7) | collective-permute-done | bytes 4128 | tf_op jit(solution)/shard_map/ppermute | solution.py:24
  33.5 2.0 %collective-permute-start.8 = (f32[10,1,128]{2,1,0:T(1,128)S(1)}, f32[10,1,128]{2,1,0:T(1,128)S(1)}, u32[]{:S(2)}, u32[]{:S(2)}) collective-permute-start(f32[10,1,128]{2,1,0:T(1,128)S(1)} %get-tuple-element.72), channel_id=1, source_target_pairs={{0,4},{4,8},{8,12},{12,0},{1,5},{5,9},{9,13},{13,1},{2,6},{6,10},{... | collective-permute-start | bytes 15368 | tf_op jit(solution)/shard_map/ppermute | solution.py:22
  35.5 1.6 %collective-permute-done.9 = f32[10,1,128]{2,1,0:T(1,128)S(1)} collective-permute-done((f32[10,1,128]{2,1,0:T(1,128)S(1)}, f32[10,1,128]{2,1,0:T(1,128)S(1)}, u32[]{:S(2)}, u32[]{:S(2)}) %collective-permute-start.9) | collective-permute-done | bytes 5152 | tf_op jit(solution)/shard_map/ppermute | solution.py:24
  37.1 1.9 %collective-permute-done.8 = f32[10,1,128]{2,1,0:T(1,128)S(1)} collective-permute-done((f32[10,1,128]{2,1,0:T(1,128)S(1)}, f32[10,1,128]{2,1,0:T(1,128)S(1)}, u32[]{:S(2)}, u32[]{:S(2)}) %collective-permute-start.8) | collective-permute-done | bytes 5152 | tf_op jit(solution)/shard_map/ppermute | solution.py:22
  41.2 2.7 %collective-permute-done.10 = f32[10,10,1]{2,1,0:T(8,128)S(1)} collective-permute-done((f32[10,10,1]{2,1,0:T(8,128)S(1)}, f32[10,10,1]{2,1,0:T(8,128)S(1)}, u32[]{:S(2)}, u32[]{:S(2)}) %collective-permute-start.10) | collective-permute-done | bytes 432 | tf_op jit(solution)/shard_map/ppermute | solution.py:22
  44.1 1.6 %collective-permute-start.13 = (f32[1,8,128]{2,1,0:T(8,128)S(1)}, f32[1,8,128]{2,1,0:T(8,128)S(1)}, u32[]{:S(2)}, u32[]{:S(2)}) collective-permute-start(f32[1,8,128]{2,1,0:T(8,128)S(1)} %get-tuple-element.79), channel_id=1, source_target_pairs={{16,0},{0,16},{17,1},{1,17},{18,2},{2,18},{19,3},{3,19},{20,4},{4,... | collective-permute-start | bytes 12296 | tf_op jit(solution)/shard_map/ppermute | solution.py:24
  46.2 1.6 %collective-permute-done.13 = f32[1,8,128]{2,1,0:T(8,128)S(1)} collective-permute-done((f32[1,8,128]{2,1,0:T(8,128)S(1)}, f32[1,8,128]{2,1,0:T(8,128)S(1)}, u32[]{:S(2)}, u32[]{:S(2)}) %collective-permute-start.13) | collective-permute-done | bytes 4128 | tf_op jit(solution)/shard_map/ppermute | solution.py:24
  47.7 1.5 %collective-permute-done.12 = f32[1,8,128]{2,1,0:T(8,128)S(1)} collective-permute-done((f32[1,8,128]{2,1,0:T(8,128)S(1)}, f32[1,8,128]{2,1,0:T(8,128)S(1)}, u32[]{:S(2)}, u32[]{:S(2)}) %collective-permute-start.12) | collective-permute-done | bytes 4128 | tf_op jit(solution)/shard_map/ppermute | solution.py:22
  49.3 2.0 %collective-permute-start.14 = (f32[10,1,128]{2,1,0:T(1,128)S(1)}, f32[10,1,128]{2,1,0:T(1,128)S(1)}, u32[]{:S(2)}, u32[]{:S(2)}) collective-permute-start(f32[10,1,128]{2,1,0:T(1,128)S(1)} %get-tuple-element.70), channel_id=1, source_target_pairs={{0,4},{4,8},{8,12},{12,0},{1,5},{5,9},{9,13},{13,1},{2,6},{6,10},{... | collective-permute-start | bytes 15368 | tf_op jit(solution)/shard_map/ppermute | solution.py:22
  51.4 1.6 %collective-permute-done.15 = f32[10,1,128]{2,1,0:T(1,128)S(1)} collective-permute-done((f32[10,1,128]{2,1,0:T(1,128)S(1)}, f32[10,1,128]{2,1,0:T(1,128)S(1)}, u32[]{:S(2)}, u32[]{:S(2)}) %collective-permute-start.15) | collective-permute-done | bytes 5152 | tf_op jit(solution)/shard_map/ppermute | solution.py:24
  52.9 1.9 %collective-permute-done.14 = f32[10,1,128]{2,1,0:T(1,128)S(1)} collective-permute-done((f32[10,1,128]{2,1,0:T(1,128)S(1)}, f32[10,1,128]{2,1,0:T(1,128)S(1)}, u32[]{:S(2)}, u32[]{:S(2)}) %collective-permute-start.14) | collective-permute-done | bytes 5152 | tf_op jit(solution)/shard_map/ppermute | solution.py:22
  55.5 2.2 %collective-permute-done.17 = f32[10,10,1]{2,1,0:T(8,128)S(1)} collective-permute-done((f32[10,10,1]{2,1,0:T(8,128)S(1)}, f32[10,10,1]{2,1,0:T(8,128)S(1)}, u32[]{:S(2)}, u32[]{:S(2)}) %collective-permute-start.17) | collective-permute-done | bytes 432 | tf_op jit(solution)/shard_map/ppermute | solution.py:24
  59.7 1.5 %collective-permute-start.18 = (f32[1,8,128]{2,1,0:T(8,128)S(1)}, f32[1,8,128]{2,1,0:T(8,128)S(1)}, u32[]{:S(2)}, u32[]{:S(2)}) collective-permute-start(f32[1,8,128]{2,1,0:T(8,128)S(1)} %get-tuple-element.76), channel_id=1, source_target_pairs={{0,16},{16,0},{1,17},{17,1},{2,18},{18,2},{3,19},{19,3},{4,20},{20... | collective-permute-start | bytes 12296 | tf_op jit(solution)/shard_map/ppermute | solution.py:22
  63.3 2.0 %collective-permute-start.20 = (f32[10,1,128]{2,1,0:T(1,128)S(1)}, f32[10,1,128]{2,1,0:T(1,128)S(1)}, u32[]{:S(2)}, u32[]{:S(2)}) collective-permute-start(f32[10,1,128]{2,1,0:T(1,128)S(1)} %get-tuple-element.68), channel_id=1, source_target_pairs={{0,4},{4,8},{8,12},{12,0},{1,5},{5,9},{9,13},{13,1},{2,6},{6,10},{... | collective-permute-start | bytes 15368 | tf_op jit(solution)/shard_map/ppermute | solution.py:22
  65.4 1.6 %collective-permute-done.21 = f32[10,1,128]{2,1,0:T(1,128)S(1)} collective-permute-done((f32[10,1,128]{2,1,0:T(1,128)S(1)}, f32[10,1,128]{2,1,0:T(1,128)S(1)}, u32[]{:S(2)}, u32[]{:S(2)}) %collective-permute-start.21) | collective-permute-done | bytes 5152 | tf_op jit(solution)/shard_map/ppermute | solution.py:24
  66.9 1.9 %collective-permute-done.20 = f32[10,1,128]{2,1,0:T(1,128)S(1)} collective-permute-done((f32[10,1,128]{2,1,0:T(1,128)S(1)}, f32[10,1,128]{2,1,0:T(1,128)S(1)}, u32[]{:S(2)}, u32[]{:S(2)}) %collective-permute-start.20) | collective-permute-done | bytes 5152 | tf_op jit(solution)/shard_map/ppermute | solution.py:22
  69.5 1.5 %collective-permute-done.23 = f32[10,10,1]{2,1,0:T(8,128)S(1)} collective-permute-done((f32[10,10,1]{2,1,0:T(8,128)S(1)}, f32[10,10,1]{2,1,0:T(8,128)S(1)}, u32[]{:S(2)}, u32[]{:S(2)}) %collective-permute-start.23) | collective-permute-done | bytes 432 | tf_op jit(solution)/shard_map/ppermute | solution.py:24
  71.0 2.6 %collective-permute-done.22 = f32[10,10,1]{2,1,0:T(8,128)S(1)} collective-permute-done((f32[10,10,1]{2,1,0:T(8,128)S(1)}, f32[10,10,1]{2,1,0:T(8,128)S(1)}, u32[]{:S(2)}, u32[]{:S(2)}) %collective-permute-start.22) | collective-permute-done | bytes 432 | tf_op jit(solution)/shard_map/ppermute | solution.py:22
  73.9 1.6 %collective-permute-start.25 = (f32[2,8,128]{2,1,0:T(8,128)S(1)}, f32[2,8,128]{2,1,0:T(8,128)S(1)}, u32[]{:S(2)}, u32[]{:S(2)}) collective-permute-start(f32[2,8,128]{2,1,0:T(8,128)S(1)} %get-tuple-element.75), channel_id=1, source_target_pairs={{16,0},{0,16},{17,1},{1,17},{18,2},{2,18},{19,3},{3,19},{20,4},{4,... | collective-permute-start | bytes 24584 | tf_op jit(solution)/shard_map/ppermute | solution.py:24
  76.0 1.6 %collective-permute-done.25 = f32[2,8,128]{2,1,0:T(8,128)S(1)} collective-permute-done((f32[2,8,128]{2,1,0:T(8,128)S(1)}, f32[2,8,128]{2,1,0:T(8,128)S(1)}, u32[]{:S(2)}, u32[]{:S(2)}) %collective-permute-start.25) | collective-permute-done | bytes 8224 | tf_op jit(solution)/shard_map/ppermute | solution.py:24
  77.6 1.5 %collective-permute-done.24 = f32[2,8,128]{2,1,0:T(8,128)S(1)} collective-permute-done((f32[2,8,128]{2,1,0:T(8,128)S(1)}, f32[2,8,128]{2,1,0:T(8,128)S(1)}, u32[]{:S(2)}, u32[]{:S(2)}) %collective-permute-start.24) | collective-permute-done | bytes 8224 | tf_op jit(solution)/shard_map/ppermute | solution.py:22
  79.2 2.0 %collective-permute-start.26 = (f32[12,2,128]{2,1,0:T(2,128)S(1)}, f32[12,2,128]{2,1,0:T(2,128)S(1)}, u32[]{:S(2)}, u32[]{:S(2)}) collective-permute-start(f32[12,2,128]{2,1,0:T(2,128)S(1)} %get-tuple-element.66), channel_id=1, source_target_pairs={{0,4},{4,8},{8,12},{12,0},{1,5},{5,9},{9,13},{13,1},{2,6},{6,10},{... | collective-permute-start | bytes 36872 | tf_op jit(solution)/shard_map/ppermute | solution.py:22
  82.8 1.9 %collective-permute-done.26 = f32[12,2,128]{2,1,0:T(2,128)S(1)} collective-permute-done((f32[12,2,128]{2,1,0:T(2,128)S(1)}, f32[12,2,128]{2,1,0:T(2,128)S(1)}, u32[]{:S(2)}, u32[]{:S(2)}) %collective-permute-start.26) | collective-permute-done | bytes 12320 | tf_op jit(solution)/shard_map/ppermute | solution.py:22
  84.9 1.7 %collective-permute-start.29 = (f32[12,12,2]{2,1,0:T(8,128)S(1)}, f32[12,12,2]{2,1,0:T(8,128)S(1)}, u32[]{:S(2)}, u32[]{:S(2)}) collective-permute-start(f32[12,12,2]{2,1,0:T(8,128)S(1)} %get-tuple-element.56), channel_id=1, source_target_pairs={{1,0},{2,1},{3,2},{0,3},{5,4},{6,5},{7,6},{4,7},{9,8},{10,9},{11,1... | collective-permute-start | bytes 3464 | tf_op jit(solution)/shard_map/ppermute | solution.py:24
  87.0 2.1 %collective-permute-done.28 = f32[12,12,2]{2,1,0:T(8,128)S(1)} collective-permute-done((f32[12,12,2]{2,1,0:T(8,128)S(1)}, f32[12,12,2]{2,1,0:T(8,128)S(1)}, u32[]{:S(2)}, u32[]{:S(2)}) %collective-permute-start.28) | collective-permute-done | bytes 1184 | tf_op jit(solution)/shard_map/ppermute | solution.py:22
  (110 shorter events, 24.6 us)
Async XLA Ops:
  1.5 5.1 %collective-permute-start.1 = (f32[6,2,8,128]{3,2,1,0:T(8,128)S(1)}, f32[6,2,8,128]{3,2,1,0:T(8,128)S(1)}, u32[]{:S(2)}, u32[]{:S(2)}) collective-permute-start(f32[6,2,8,128]{3,2,1,0:T(8,128)S(1)} %get-tuple-element.43), channel_id=1, source_target_pairs={{16,0},{0,16},{17,1},{1,17},{18,2},{2,18},{19,3},{3,19},{20,4},{4,... | collective-permute-start | bytes 147464 | tf_op jit(solution)/shard_map/ppermute | solution.py:24
  4.5 15.0 %copy-start.2 = (f32[8,8,128]{2,1,0:T(8,128)S(1)}, f32[8,8,128]{2,1,0:T(8,128)}, u32[]{:S(2)}) copy-start(f32[8,8,128]{2,1,0:T(8,128)} %param.3) | copy-start | bytes 98308
  4.5 4.1 %collective-permute-start = (f32[6,2,8,128]{3,2,1,0:T(8,128)S(1)}, f32[6,2,8,128]{3,2,1,0:T(8,128)S(1)}, u32[]{:S(2)}, u32[]{:S(2)}) collective-permute-start(f32[6,2,8,128]{3,2,1,0:T(8,128)S(1)} %get-tuple-element.42), channel_id=1, source_target_pairs={{0,16},{16,0},{1,17},{17,1},{2,18},{18,2},{3,19},{19,3},{4,20},{20... | collective-permute-start | bytes 147464 | tf_op jit(solution)/shard_map/ppermute | solution.py:22
  9.7 5.6 %collective-permute-start.3 = (f32[6,12,2,128]{3,2,1,0:T(2,128)S(1)}, f32[6,12,2,128]{3,2,1,0:T(2,128)S(1)}, u32[]{:S(2)}, u32[]{:S(2)}) collective-permute-start(f32[6,12,2,128]{3,2,1,0:T(2,128)S(1)} %get-tuple-element.37), channel_id=1, source_target_pairs={{4,0},{8,4},{12,8},{0,12},{5,1},{9,5},{13,9},{1,13},{6,2},{10,6},{... | collective-permute-start | bytes 221192 | tf_op jit(solution)/shard_map/ppermute | solution.py:24
  13.4 6.2 %collective-permute-start.2 = (f32[6,12,2,128]{3,2,1,0:T(2,128)S(1)}, f32[6,12,2,128]{3,2,1,0:T(2,128)S(1)}, u32[]{:S(2)}, u32[]{:S(2)}) collective-permute-start(f32[6,12,2,128]{3,2,1,0:T(2,128)S(1)} %get-tuple-element.36), channel_id=1, source_target_pairs={{0,4},{4,8},{8,12},{12,0},{1,5},{5,9},{9,13},{13,1},{2,6},{6,10},{... | collective-permute-start | bytes 221192 | tf_op jit(solution)/shard_map/ppermute | solution.py:22
  20.4 2.0 %collective-permute-start.5 = (f32[6,12,12,2]{2,3,1,0:T(2,128)S(1)}, f32[6,12,12,2]{2,3,1,0:T(2,128)S(1)}, u32[]{:S(2)}, u32[]{:S(2)}) collective-permute-start(f32[6,12,12,2]{2,3,1,0:T(2,128)S(1)} %copy.68), channel_id=1, source_target_pairs={{1,0},{2,1},{3,2},{0,3},{5,4},{6,5},{7,6},{4,7},{9,8},{10,9},{11,1... | collective-permute-start | bytes 20744 | tf_op jit(solution)/shard_map/ppermute | solution.py:24
  21.6 4.1 %collective-permute-start.4 = (f32[6,12,12,2]{2,3,1,0:T(2,128)}, f32[6,12,12,2]{2,3,1,0:T(2,128)}, u32[]{:S(2)}, u32[]{:S(2)}) collective-permute-start(f32[6,12,12,2]{2,3,1,0:T(2,128)} %copy.67), channel_id=1, source_target_pairs={{0,1},{1,2},{2,3},{3,0},{4,5},{5,6},{6,7},{7,4},{8,9},{9,10},{10,1... | collective-permute-start | bytes 20744 | tf_op jit(solution)/shard_map/ppermute | solution.py:22
  29.2 3.7 %collective-permute-start.7 = (f32[1,8,128]{2,1,0:T(8,128)S(1)}, f32[1,8,128]{2,1,0:T(8,128)S(1)}, u32[]{:S(2)}, u32[]{:S(2)}) collective-permute-start(f32[1,8,128]{2,1,0:T(8,128)S(1)} %get-tuple-element.81), channel_id=1, source_target_pairs={{16,0},{0,16},{17,1},{1,17},{18,2},{2,18},{19,3},{3,19},{20,4},{4,... | collective-permute-start | bytes 12296 | tf_op jit(solution)/shard_map/ppermute | solution.py:24
  29.8 3.6 %collective-permute-start.6 = (f32[1,8,128]{2,1,0:T(8,128)S(1)}, f32[1,8,128]{2,1,0:T(8,128)S(1)}, u32[]{:S(2)}, u32[]{:S(2)}) collective-permute-start(f32[1,8,128]{2,1,0:T(8,128)S(1)} %get-tuple-element.80), channel_id=1, source_target_pairs={{0,16},{16,0},{1,17},{17,1},{2,18},{18,2},{3,19},{19,3},{4,20},{20... | collective-permute-start | bytes 12296 | tf_op jit(solution)/shard_map/ppermute | solution.py:22
  33.4 3.7 %collective-permute-start.9 = (f32[10,1,128]{2,1,0:T(1,128)S(1)}, f32[10,1,128]{2,1,0:T(1,128)S(1)}, u32[]{:S(2)}, u32[]{:S(2)}) collective-permute-start(f32[10,1,128]{2,1,0:T(1,128)S(1)} %get-tuple-element.73), channel_id=1, source_target_pairs={{4,0},{8,4},{12,8},{0,12},{5,1},{9,5},{13,9},{1,13},{6,2},{10,6},{... | collective-permute-start | bytes 15368 | tf_op jit(solution)/shard_map/ppermute | solution.py:24
  33.5 5.5 %collective-permute-start.8 = (f32[10,1,128]{2,1,0:T(1,128)S(1)}, f32[10,1,128]{2,1,0:T(1,128)S(1)}, u32[]{:S(2)}, u32[]{:S(2)}) collective-permute-start(f32[10,1,128]{2,1,0:T(1,128)S(1)} %get-tuple-element.72), channel_id=1, source_target_pairs={{0,4},{4,8},{8,12},{12,0},{1,5},{5,9},{9,13},{13,1},{2,6},{6,10},{... | collective-permute-start | bytes 15368 | tf_op jit(solution)/shard_map/ppermute | solution.py:22
  39.0 2.1 %collective-permute-start.11 = (f32[10,10,1]{2,1,0:T(8,128)S(1)}, f32[10,10,1]{2,1,0:T(8,128)S(1)}, u32[]{:S(2)}, u32[]{:S(2)}) collective-permute-start(f32[10,10,1]{2,1,0:T(8,128)S(1)} %get-tuple-element.63), channel_id=1, source_target_pairs={{1,0},{2,1},{3,2},{0,3},{5,4},{6,5},{7,6},{4,7},{9,8},{10,9},{11,1... | collective-permute-start | bytes 1208 | tf_op jit(solution)/shard_map/ppermute | solution.py:24
  39.1 4.8 %collective-permute-start.10 = (f32[10,10,1]{2,1,0:T(8,128)S(1)}, f32[10,10,1]{2,1,0:T(8,128)S(1)}, u32[]{:S(2)}, u32[]{:S(2)}) collective-permute-start(f32[10,10,1]{2,1,0:T(8,128)S(1)} %get-tuple-element.62), channel_id=1, source_target_pairs={{0,1},{1,2},{2,3},{3,0},{4,5},{5,6},{6,7},{7,4},{8,9},{9,10},{10,1... | collective-permute-start | bytes 1208 | tf_op jit(solution)/shard_map/ppermute | solution.py:22
  44.1 3.7 %collective-permute-start.13 = (f32[1,8,128]{2,1,0:T(8,128)S(1)}, f32[1,8,128]{2,1,0:T(8,128)S(1)}, u32[]{:S(2)}, u32[]{:S(2)}) collective-permute-start(f32[1,8,128]{2,1,0:T(8,128)S(1)} %get-tuple-element.79), channel_id=1, source_target_pairs={{16,0},{0,16},{17,1},{1,17},{18,2},{2,18},{19,3},{3,19},{20,4},{4,... | collective-permute-start | bytes 12296 | tf_op jit(solution)/shard_map/ppermute | solution.py:24
  45.6 3.6 %collective-permute-start.12 = (f32[1,8,128]{2,1,0:T(8,128)S(1)}, f32[1,8,128]{2,1,0:T(8,128)S(1)}, u32[]{:S(2)}, u32[]{:S(2)}) collective-permute-start(f32[1,8,128]{2,1,0:T(8,128)S(1)} %get-tuple-element.78), channel_id=1, source_target_pairs={{0,16},{16,0},{1,17},{17,1},{2,18},{18,2},{3,19},{19,3},{4,20},{20... | collective-permute-start | bytes 12296 | tf_op jit(solution)/shard_map/ppermute | solution.py:22
  49.3 3.7 %collective-permute-start.15 = (f32[10,1,128]{2,1,0:T(1,128)S(1)}, f32[10,1,128]{2,1,0:T(1,128)S(1)}, u32[]{:S(2)}, u32[]{:S(2)}) collective-permute-start(f32[10,1,128]{2,1,0:T(1,128)S(1)} %get-tuple-element.71), channel_id=1, source_target_pairs={{4,0},{8,4},{12,8},{0,12},{5,1},{9,5},{13,9},{1,13},{6,2},{10,6},{... | collective-permute-start | bytes 15368 | tf_op jit(solution)/shard_map/ppermute | solution.py:24
  49.3 5.5 %collective-permute-start.14 = (f32[10,1,128]{2,1,0:T(1,128)S(1)}, f32[10,1,128]{2,1,0:T(1,128)S(1)}, u32[]{:S(2)}, u32[]{:S(2)}) collective-permute-start(f32[10,1,128]{2,1,0:T(1,128)S(1)} %get-tuple-element.70), channel_id=1, source_target_pairs={{0,4},{4,8},{8,12},{12,0},{1,5},{5,9},{9,13},{13,1},{2,6},{6,10},{... | collective-permute-start | bytes 15368 | tf_op jit(solution)/shard_map/ppermute | solution.py:22
  54.9 2.8 %collective-permute-start.17 = (f32[10,10,1]{2,1,0:T(8,128)S(1)}, f32[10,10,1]{2,1,0:T(8,128)S(1)}, u32[]{:S(2)}, u32[]{:S(2)}) collective-permute-start(f32[10,10,1]{2,1,0:T(8,128)S(1)} %get-tuple-element.61), channel_id=1, source_target_pairs={{1,0},{2,1},{3,2},{0,3},{5,4},{6,5},{7,6},{4,7},{9,8},{10,9},{11,1... | collective-permute-start | bytes 1208 | tf_op jit(solution)/shard_map/ppermute | solution.py:24
  55.0 3.9 %collective-permute-start.16 = (f32[10,10,1]{2,1,0:T(8,128)S(1)}, f32[10,10,1]{2,1,0:T(8,128)S(1)}, u32[]{:S(2)}, u32[]{:S(2)}) collective-permute-start(f32[10,10,1]{2,1,0:T(8,128)S(1)} %get-tuple-element.60), channel_id=1, source_target_pairs={{0,1},{1,2},{2,3},{3,0},{4,5},{5,6},{6,7},{7,4},{8,9},{9,10},{10,1... | collective-permute-start | bytes 1208 | tf_op jit(solution)/shard_map/ppermute | solution.py:22
  59.1 3.7 %collective-permute-start.19 = (f32[1,8,128]{2,1,0:T(8,128)S(1)}, f32[1,8,128]{2,1,0:T(8,128)S(1)}, u32[]{:S(2)}, u32[]{:S(2)}) collective-permute-start(f32[1,8,128]{2,1,0:T(8,128)S(1)} %get-tuple-element.77), channel_id=1, source_target_pairs={{16,0},{0,16},{17,1},{1,17},{18,2},{2,18},{19,3},{3,19},{20,4},{4,... | collective-permute-start | bytes 12296 | tf_op jit(solution)/shard_map/ppermute | solution.py:24
  59.7 3.6 %collective-permute-start.18 = (f32[1,8,128]{2,1,0:T(8,128)S(1)}, f32[1,8,128]{2,1,0:T(8,128)S(1)}, u32[]{:S(2)}, u32[]{:S(2)}) collective-permute-start(f32[1,8,128]{2,1,0:T(8,128)S(1)} %get-tuple-element.76), channel_id=1, source_target_pairs={{0,16},{16,0},{1,17},{17,1},{2,18},{18,2},{3,19},{19,3},{4,20},{20... | collective-permute-start | bytes 12296 | tf_op jit(solution)/shard_map/ppermute | solution.py:22
  63.3 3.7 %collective-permute-start.21 = (f32[10,1,128]{2,1,0:T(1,128)S(1)}, f32[10,1,128]{2,1,0:T(1,128)S(1)}, u32[]{:S(2)}, u32[]{:S(2)}) collective-permute-start(f32[10,1,128]{2,1,0:T(1,128)S(1)} %get-tuple-element.69), channel_id=1, source_target_pairs={{4,0},{8,4},{12,8},{0,12},{5,1},{9,5},{13,9},{1,13},{6,2},{10,6},{... | collective-permute-start | bytes 15368 | tf_op jit(solution)/shard_map/ppermute | solution.py:24
  63.3 5.5 %collective-permute-start.20 = (f32[10,1,128]{2,1,0:T(1,128)S(1)}, f32[10,1,128]{2,1,0:T(1,128)S(1)}, u32[]{:S(2)}, u32[]{:S(2)}) collective-permute-start(f32[10,1,128]{2,1,0:T(1,128)S(1)} %get-tuple-element.68), channel_id=1, source_target_pairs={{0,4},{4,8},{8,12},{12,0},{1,5},{5,9},{9,13},{13,1},{2,6},{6,10},{... | collective-permute-start | bytes 15368 | tf_op jit(solution)/shard_map/ppermute | solution.py:22
  68.9 2.1 %collective-permute-start.23 = (f32[10,10,1]{2,1,0:T(8,128)S(1)}, f32[10,10,1]{2,1,0:T(8,128)S(1)}, u32[]{:S(2)}, u32[]{:S(2)}) collective-permute-start(f32[10,10,1]{2,1,0:T(8,128)S(1)} %get-tuple-element.59), channel_id=1, source_target_pairs={{1,0},{2,1},{3,2},{0,3},{5,4},{6,5},{7,6},{4,7},{9,8},{10,9},{11,1... | collective-permute-start | bytes 1208 | tf_op jit(solution)/shard_map/ppermute | solution.py:24
  69.0 4.7 %collective-permute-start.22 = (f32[10,10,1]{2,1,0:T(8,128)S(1)}, f32[10,10,1]{2,1,0:T(8,128)S(1)}, u32[]{:S(2)}, u32[]{:S(2)}) collective-permute-start(f32[10,10,1]{2,1,0:T(8,128)S(1)} %get-tuple-element.58), channel_id=1, source_target_pairs={{0,1},{1,2},{2,3},{3,0},{4,5},{5,6},{6,7},{7,4},{8,9},{9,10},{10,1... | collective-permute-start | bytes 1208 | tf_op jit(solution)/shard_map/ppermute | solution.py:22
  73.8 15.4 %copy-start.1 = (f32[8,8,128]{2,1,0:T(8,128)}, f32[8,8,128]{2,1,0:T(8,128)S(1)}, u32[]{:S(2)}) copy-start(f32[8,8,128]{2,1,0:T(8,128)S(1)} %fusion.71) | copy-start | bytes 98308
  73.9 3.7 %collective-permute-start.25 = (f32[2,8,128]{2,1,0:T(8,128)S(1)}, f32[2,8,128]{2,1,0:T(8,128)S(1)}, u32[]{:S(2)}, u32[]{:S(2)}) collective-permute-start(f32[2,8,128]{2,1,0:T(8,128)S(1)} %get-tuple-element.75), channel_id=1, source_target_pairs={{16,0},{0,16},{17,1},{1,17},{18,2},{2,18},{19,3},{3,19},{20,4},{4,... | collective-permute-start | bytes 24584 | tf_op jit(solution)/shard_map/ppermute | solution.py:24
  75.4 3.7 %collective-permute-start.24 = (f32[2,8,128]{2,1,0:T(8,128)S(1)}, f32[2,8,128]{2,1,0:T(8,128)S(1)}, u32[]{:S(2)}, u32[]{:S(2)}) collective-permute-start(f32[2,8,128]{2,1,0:T(8,128)S(1)} %get-tuple-element.74), channel_id=1, source_target_pairs={{0,16},{16,0},{1,17},{17,1},{2,18},{18,2},{3,19},{19,3},{4,20},{20... | collective-permute-start | bytes 24584 | tf_op jit(solution)/shard_map/ppermute | solution.py:22
  79.1 3.7 %collective-permute-start.27 = (f32[12,2,128]{2,1,0:T(2,128)S(1)}, f32[12,2,128]{2,1,0:T(2,128)S(1)}, u32[]{:S(2)}, u32[]{:S(2)}) collective-permute-start(f32[12,2,128]{2,1,0:T(2,128)S(1)} %get-tuple-element.67), channel_id=1, source_target_pairs={{4,0},{8,4},{12,8},{0,12},{5,1},{9,5},{13,9},{1,13},{6,2},{10,6},{... | collective-permute-start | bytes 36872 | tf_op jit(solution)/shard_map/ppermute | solution.py:24
  79.2 5.5 %collective-permute-start.26 = (f32[12,2,128]{2,1,0:T(2,128)S(1)}, f32[12,2,128]{2,1,0:T(2,128)S(1)}, u32[]{:S(2)}, u32[]{:S(2)}) collective-permute-start(f32[12,2,128]{2,1,0:T(2,128)S(1)} %get-tuple-element.66), channel_id=1, source_target_pairs={{0,4},{4,8},{8,12},{12,0},{1,5},{5,9},{9,13},{13,1},{2,6},{6,10},{... | collective-permute-start | bytes 36872 | tf_op jit(solution)/shard_map/ppermute | solution.py:22
  84.8 4.2 %collective-permute-start.28 = (f32[12,12,2]{2,1,0:T(8,128)S(1)}, f32[12,12,2]{2,1,0:T(8,128)S(1)}, u32[]{:S(2)}, u32[]{:S(2)}) collective-permute-start(f32[12,12,2]{2,1,0:T(8,128)S(1)} %get-tuple-element.57), channel_id=1, source_target_pairs={{0,1},{1,2},{2,3},{3,0},{4,5},{5,6},{6,7},{7,4},{8,9},{9,10},{10,1... | collective-permute-start | bytes 3464 | tf_op jit(solution)/shard_map/ppermute | solution.py:22
  84.9 4.2 %collective-permute-start.29 = (f32[12,12,2]{2,1,0:T(8,128)S(1)}, f32[12,12,2]{2,1,0:T(8,128)S(1)}, u32[]{:S(2)}, u32[]{:S(2)}) collective-permute-start(f32[12,12,2]{2,1,0:T(8,128)S(1)} %get-tuple-element.56), channel_id=1, source_target_pairs={{1,0},{2,1},{3,2},{0,3},{5,4},{6,5},{7,6},{4,7},{9,8},{10,9},{11,1... | collective-permute-start | bytes 3464 | tf_op jit(solution)/shard_map/ppermute | solution.py:24
  (1 other events, 15.0 us)
where the time goes:
time: 90.8 us; the launch traced here: 90.3 us
  waiting for transfers between devices  48.7 us (54%)
  starting transfers between devices  27.4 us (30%)
  other arithmetic  8.34 us (9%)
  local copies, waits for them, and re-layouts  4.71 us (5%)
  between operations  1.11 us (1%)
    ppermute x15, waiting for transfers between devices, extended(): lax.ppermute(tail, axis, [(i, (i + 1) % count) for i in range(count)])  29 us
    ppermute x15, waiting for transfers between devices, extended(): lax.ppermute(head, axis, [((i + 1) % count, i) for i in range(count)])  19.7 us
    ppermute x15, starting transfers between devices, extended(): lax.ppermute(tail, axis, [(i, (i + 1) % count) for i in range(count)])  14.2 us
    ppermute x15, starting transfers between devices, extended(): lax.ppermute(head, axis, [((i + 1) % count, i) for i in range(count)])  13.2 us
    concatenate x9, other arithmetic, extended(): jnp.concatenate([lax.ppermute(tail, axis, [(i, (i + 1) % count) for i in...  2.25 us
    slice x6, other arithmetic, extended(): lax.slice_in_dim(cells, cells.shape[dim] - width, cells.shape[dim], axis=...  1.96 us
  transfers between devices with their start and end apart: 30, of which 28 were waited for; matrix products, arithmetic and copies ran while one was open for 5% of the time, Pallas kernels for 0%

commit v1 on v0

v1 whole, which is shorter than its diff:
```python
import functools
import itertools

import jax
import jax.numpy as jnp
from jax import lax
from jax.experimental import pallas as pl
from jax.experimental.pallas import tpu as pltpu
from jax.sharding import PartitionSpec as P

SWEEPS = 4
ALPHA = 10.0
GAMMA = 1.4
LAMBDA = 3.0
STEP_DT = 0.4
MESH = pl.DeviceIdType.MESH
AXES = ("gx", "gy", "gz")

OFFSETS = [o for o in itertools.product((-1, 0, 1), repeat=3) if 1 <= sum(abs(v) for v in o) <= 2]
NEAR = [o for o in OFFSETS if sum(abs(v) for v in o) == 1]
Z_MOVES = [o for o in OFFSETS if o[2] != 0]
XY_MOVES = [o for o in OFFSETS if o[0] != 0 and o[1] != 0]


def neg(offset):
    return tuple(-v for v in offset)


def iota(shape, dim):
    return lax.broadcasted_iota(jnp.int32, shape, dim)


def roll(value, shift, axis):
    size = value.shape[axis]
    shift = shift % size
    return value if shift == 0 else pltpu.roll(value, shift, axis)


def ring(core, ghost, step, axis):
    size = core.shape[axis]
    a, b = roll(core, -step, axis), roll(ghost, -step, axis)
    edge = iota(core.shape, axis) == (size - 1 if step == 1 else 0)
    return jnp.where(edge, b, a), jnp.where(edge, a, b)


def kernel(sizes, cons_hbm, sig_hbm, adv_ref, out_sig_ref, cons, sig,
           y1s, z1s, d1s, xm1r, xs1r, y1r, z1r, d1r,
           s2, y2s, z2s, x2r, y2r, z2r, d2r,
           y3s, z3s, x3r, y3r, z3r,
           in_sem, send_sem, recv_sem):
    X, R, L = sig.shape
    me = [lax.axis_index(a) for a in AXES]
    G = X // 4

    def device(offset):
        return {a: lax.rem(me[i] + offset[i] + sizes[i], sizes[i]) for i, a in enumerate(AXES)}

    load_c = pltpu.make_async_copy(cons_hbm, cons, in_sem.at[0])
    load_s = pltpu.make_async_copy(sig_hbm, sig, in_sem.at[1])
    load_c.start()
    load_s.start()
    barrier = pltpu.get_barrier_semaphore()
    for o in OFFSETS:
        pl.semaphore_signal(barrier, inc=1, device_id=device(o), device_id_type=MESH)

    sent = []
    count = [0]

    def send(src, dst, offset):
        n = count[0]
        count[0] += 1
        copy = pltpu.make_async_remote_copy(
            src_ref=src, dst_ref=dst, send_sem=send_sem.at[n], recv_sem=recv_sem.at[n],
            device_id=device(offset), device_id_type=MESH)
        copy.start()
        sent.append(copy)
        return copy

    rows = lambda shape: iota(shape, len(shape) - 2)
    lanes = lambda shape: iota(shape, len(shape) - 1)

    def pack_rows(field, first):
        out = field[0:G]
        r = rows(out.shape)
        for g in range(1, 4):
            part = roll(field[g * G:(g + 1) * G], 2 * g, 1)
            at = (first + 2 * g) % R
            out = jnp.where((r == at) | (r == at + 1), part, out)
        return out

    def unpack_rows(after, before):
        parts = []
        low = rows(after.shape) < R // 2
        for g in range(4):
            parts.append(jnp.where(low, roll(after, -2 * g, 1), roll(before, -2 * g, 1)))
        return jnp.concatenate(parts, axis=0)

    def pack_lanes(fields):
        tiles = [f[p] for f in fields for p in range(X)]
        out = jnp.zeros((R, L), jnp.float32)
        lane = lanes((R, L))
        for k, tile in enumerate(tiles):
            out = jnp.where(((lane + 2) % L) // 4 == k, roll(tile, 4 * k, 1), out)
        return out

    def merge_lanes(after, before):
        return jnp.where(lanes(after.shape) % 4 < 2, after, before)

    def unpack_lanes(packed, k):
        return roll(packed, -4 * k, 1)

    load_c.wait()
    load_s.wait()
    pl.semaphore_wait(barrier, len(OFFSETS))
    x1 = []
    for j, (dx, lo) in enumerate(((1, X - 2), (-1, 0))):
        x1.append(send(cons.at[0:4, lo:lo + 2], xm1r.at[j, 0:4], (dx, 0, 0)))
        x1.append(send(sig.at[lo:lo + 2], xs1r.at[j], (dx, 0, 0)))
    C0 = [cons[f] for f in range(4)] + [sig[...], cons[4]]
    for f in range(5):
        y1s[0, f] = pack_rows(C0[f], R - 2)
        y1s[1, f] = pack_rows(C0[f], 0)
    y1 = []
    for j, dy in enumerate((1, -1)):
        y1.append(send(y1s.at[j, 0:5], y1r.at[j, 0:5], (0, dy, 0)))
    z1s[0] = pack_lanes(C0[0:4])
    z1s[1] = pack_lanes(C0[4:6])
    row2 = rows((R, L))
    for n, (dx, dy, _) in enumerate(XY_MOVES):
        p = X - 1 if dx == 1 else 0
        src = R - 1 if dy == 1 else 0
        out = C0[0][p]
        for f in range(1, 5):
            out = jnp.where(row2 == (src + f) % R, roll(C0[f][p], f, 0), out)
        d1s[n] = out
    d1 = [send(d1s.at[n], d1r.at[n], o) for n, o in enumerate(XY_MOVES)]
    z1 = [send(z1s, z1r.at[n], o) for n, o in enumerate(Z_MOVES)]
    late = []
    for j, (dx, lo) in enumerate(((1, X - 2), (-1, 0))):
        late.append(send(cons.at[4, lo:lo + 2], xm1r.at[j, 4], (dx, 0, 0)))
    y1s[0, 5] = pack_rows(C0[5], R - 2)
    y1s[1, 5] = pack_rows(C0[5], 0)
    for j, dy in enumerate((1, -1)):
        late.append(send(y1s.at[j, 5], y1r.at[j, 5], (0, dy, 0)))
    for copy in x1 + y1 + d1 + z1:
        copy.wait_recv()

    def z_from(buf, dx, dy):
        return merge_lanes(buf[Z_MOVES.index((-dx, -dy, -1))], buf[Z_MOVES.index((-dx, -dy, 1))])

    def grown(core, xlo, xhi, y, zpack, f, dlo, dhi):
        c = jnp.concatenate([xlo, core, xhi], axis=0)
        y = jnp.concatenate([dlo[None], y, dhi[None]], axis=0)
        here, below, above, diag = zpack
        z = [unpack_lanes(below, f * X + X - 1)]
        z += [unpack_lanes(here, f * X + p) for p in range(X)]
        z += [unpack_lanes(above, f * X)]
        w = [unpack_lanes(diag, f * X + p) for p in range(X)]
        stack = lambda t: jnp.concatenate([v[None] for v in t], axis=0)
        return c, y, stack(z), stack(w)

    def z_packs(buf):
        low = rows(buf.shape[1:]) < R // 2
        return (z_from(buf, 0, 0), z_from(buf, -1, 0), z_from(buf, 1, 0),
                jnp.where(low, z_from(buf, 0, 1), z_from(buf, 0, -1)))

    packs = z_packs(z1r)
    low2 = row2 < R // 2

    def corner(buf, dx, f):
        after = buf[XY_MOVES.index((-dx, -1, 0))]
        before = buf[XY_MOVES.index((-dx, 1, 0))]
        return jnp.where(low2, roll(after, -f, 0), roll(before, -f, 0))

    ext = []
    for f in range(5):
        zp = tuple(v[0 if f < 4 else 1] for v in packs)
        xlo, xhi = (xm1r[0, f], xm1r[1, f]) if f < 4 else (xs1r[0], xs1r[1])
        yy = unpack_rows(y1r[1, f], y1r[0, f])
        ext.append(grown(C0[f], xlo, xhi, yy, zp, f % 4, corner(d1r, -1, f), corner(d1r, 1, f)))

    def around(field):
        c, y, z, w = field
        cm = c[1:X + 3]
        yp, ym = ring(cm, y, 1, 1), ring(cm, y, -1, 1)
        zp, zm = ring(cm, z, 1, 2), ring(cm, z, -1, 2)
        zy_p, zy_m = ring(z[1:X + 1], w, 1, 1)[0], ring(z[1:X + 1], w, -1, 1)[0]
        yz_p, yz_m = ring(y[1:X + 1], w, 1, 2)[0], ring(y[1:X + 1], w, -1, 2)[0]
        core = [(c[2:X + 4], c[0:X + 2]), (yp[0], ym[0]), (zp[0], zm[0])]
        yt = [(y[2:X + 2], y[0:X]), (yp[1][1:X + 1], ym[1][1:X + 1]), (yz_p, yz_m)]
        zt = [(z[2:X + 2], z[0:X]), (zy_p, zy_m), (zp[1][1:X + 1], zm[1][1:X + 1])]
        return core, yt, zt

    def middle(field):
        c, y, z, _ = field
        return c[1:X + 3], y[1:X + 1], z[1:X + 1]

    inv = tuple(1.0 / v for v in ext[0])
    vel = [tuple(m * r for m, r in zip(ext[k], inv)) for k in (1, 2, 3)]
    vel_n = [around(v) for v in vel]
    inv_n = around(inv)
    inv_m = middle(inv)
    source, weight, scale = [], [], []
    for t in range(3):
        g = [[0.5 * (vel_n[k][t][d][0] - vel_n[k][t][d][1]) for d in range(3)] for k in range(3)]
        div = g[0][0] + g[1][1] + g[2][2]
        source.append(g[0][0] * g[0][0] + g[1][1] * g[1][1] + g[2][2] * g[2][2]
                      + 2.0 * (g[0][1] * g[1][0] + g[0][2] * g[2][0] + g[1][2] * g[2][1]) + div * div)
        ws = [[0.5 * (inv_m[t] + inv_n[t][d][s]) for s in range(2)] for d in range(3)]
        total = sum(w for pair in ws for w in pair)
        weight.append(ws)
        scale.append(ALPHA / (inv_m[t] + ALPHA * total))

    def update(nbr, t, cut=None):
        take = (lambda v: v) if cut is None else (lambda v: v[cut])
        acc = take(source[t])
        for d in range(3):
            for s in range(2):
                acc = acc + take(weight[t][d][s]) * nbr[d][s]
        return acc * take(scale[t])

    def core_sweep(c, y, z):
        m = c[1:X + 1]
        nbr = [(c[2:X + 2], c[0:X]),
               (ring(m, y, 1, 1)[0], ring(m, y, -1, 1)[0]),
               (ring(m, z, 1, 2)[0], ring(m, z, -1, 2)[0])]
        return update(nbr, 0, slice(1, X + 1))

    def two_sweeps(field):
        n = around(field)
        c, y, z = (update(n[t], t) for t in range(3))
        return core_sweep(c, y, z)

    sigma2 = two_sweeps(ext[4])
    s2[...] = sigma2
    y2s[0] = pack_rows(sigma2, R - 2)
    y2s[1] = pack_rows(sigma2, 0)
    z2s[...] = pack_lanes([sigma2])
    got2 = []
    for j, dy in enumerate((1, -1)):
        got2.append(send(y2s.at[j], y2r.at[j], (0, dy, 0)))
    for n, o in enumerate(XY_MOVES):
        got2.append(send(s2.at[X - 1 if o[0] == 1 else 0], d2r.at[n], o))
    for n, o in enumerate(Z_MOVES):
        got2.append(send(z2s, z2r.at[n], o))
    for j, (dx, lo) in enumerate(((1, X - 2), (-1, 0))):
        got2.append(send(s2.at[lo:lo + 2], x2r.at[j], (dx, 0, 0)))

    for copy in late:
        copy.wait_recv()
    order = (0, 1, 2, 3)
    xc = [ext[f][0] for f in order] + [jnp.concatenate([xm1r[0, 4], C0[5], xm1r[1, 4]], axis=0)]
    yc = [ext[f][1][1:X + 1] for f in order] + [unpack_rows(y1r[1, 5], y1r[0, 5])]
    zc = [ext[f][2][1:X + 1] for f in order] + [
        jnp.concatenate([unpack_lanes(packs[0][1], X + p)[None] for p in range(X)], axis=0)]
    core = C0[0:4] + [C0[5]]

    def x_stencil(c):
        return c[0:X + 1], c[1:X + 2], c[2:X + 3], c[3:X + 4]

    def ring_stencil(c, g, axis):
        m, p = ring(c, g, -1, axis), ring(c, g, 1, axis)
        pp = ring(p[0], p[1], 1, axis)
        cat = lambda a, b: jnp.concatenate([a, b], axis=0)
        return cat(*m), cat(c, g), cat(*p), cat(*pp)

    def faces(st):
        m, q, p, pp = st
        sixth = 1.0 / 6.0
        return (5.0 * q + 2.0 * p - m) * sixth, (2.0 * q + 5.0 * p - pp) * sixth

    def plain_flux(s, d):
        r = 1.0 / s[0]
        v = s[1 + d] * r
        pressure = (GAMMA - 1.0) * (s[4] - 0.5 * (s[1] * s[1] + s[2] * s[2] + s[3] * s[3]) * r)
        out = [s[1 + d]]
        for k in range(3):
            out.append(s[1 + k] * v + pressure if k == d else s[1 + k] * v)
        out.append((s[4] + pressure) * v)
        return out, v

    def difference(flux, d):
        if d == 0:
            return flux[1:X + 1] - flux[0:X]
        return flux[0:X] - ring(flux[0:X], flux[X:2 * X], -1, d)[0]

    base = [None] * 5
    speed = []
    for d in range(3):
        if d == 0:
            lr = [faces(x_stencil(c)) for c in xc]
        else:
            lr = [faces(ring_stencil(c, g, d)) for c, g in zip(core, (None, yc, zc)[d])]
        lf, lv = plain_flux([v[0] for v in lr], d)
        rf, rv = plain_flux([v[1] for v in lr], d)
        speed.append((lv, rv))
        for k in range(5):
            flux = 0.5 * (lf[k] + rf[k]) - (0.5 * LAMBDA) * (lr[k][1] - lr[k][0])
            change = difference(flux, d)
            base[k] = change if base[k] is None else base[k] + change
    base = [core[k] - STEP_DT * base[k] for k in range(5)]
    adv_ref[0] = base[0]

    for copy in got2:
        copy.wait_recv()
    zp2 = z_packs(z2r)
    c2 = jnp.concatenate([x2r[0], sigma2, x2r[1]], axis=0)
    sigma4 = two_sweeps(grown(sigma2, x2r[0], x2r[1], unpack_rows(y2r[1], y2r[0]), zp2, 0,
                              corner(d2r, -1, 0), corner(d2r, 1, 0)))

    out_sig_ref[...] = sigma4
    y3s[0] = pack_rows(sigma4, R - 2)
    y3s[1] = pack_rows(sigma4, 0)
    z3s[...] = pack_lanes([sigma4])
    got3 = []
    for j, dy in enumerate((1, -1)):
        got3.append(send(y3s.at[j], y3r.at[j], (0, dy, 0)))
    for j, dz in enumerate((1, -1)):
        got3.append(send(z3s, z3r.at[j], (0, 0, dz)))
    for j, (dx, lo) in enumerate(((1, X - 2), (-1, 0))):
        got3.append(send(out_sig_ref.at[lo:lo + 2], x3r.at[j], (dx, 0, 0)))
    for copy in got3:
        copy.wait_recv()
    y3 = unpack_rows(y3r[1], y3r[0])
    zpk = merge_lanes(z3r[1], z3r[0])
    z3 = jnp.concatenate([unpack_lanes(zpk, p)[None] for p in range(X)], axis=0)
    x3 = jnp.concatenate([x3r[0], sigma4, x3r[1]], axis=0)
    energy = base[4]
    for d in range(3):
        st = x_stencil(x3) if d == 0 else ring_stencil(sigma4, y3 if d == 1 else z3, d)
        ls, rs = faces(st)
        lv, rv = speed[d]
        adv_ref[1 + d] = base[1 + d] - (0.5 * STEP_DT) * difference(ls + rs, d)
        energy = energy - (0.5 * STEP_DT) * difference(ls * lv + rs * rv, d)
    adv_ref[4] = energy
    for copy in sent:
        copy.wait_send()


def solution(mesh):
    sizes = tuple(mesh.shape[a] for a in AXES)

    def on_device(conserved, sigma_guess):
        X, R, L = sigma_guess.shape
        G = X // 4
        f32 = jnp.float32
        vm = lambda *shape: pltpu.VMEM(shape, f32)
        nz, nd = len(Z_MOVES), len(XY_MOVES)
        messages = 48
        return pl.pallas_call(
            functools.partial(kernel, sizes),
            out_shape=(jax.ShapeDtypeStruct(conserved.shape, f32), jax.ShapeDtypeStruct(sigma_guess.shape, f32)),
            in_specs=[pl.BlockSpec(memory_space=pl.ANY)] * 2,
            out_specs=(pl.BlockSpec(memory_space=pltpu.VMEM),) * 2,
            scratch_shapes=[
                vm(*conserved.shape), vm(X, R, L),
                vm(2, 6, G, R, L), vm(2, R, L), vm(nd, R, L),
                vm(2, 5, 2, R, L), vm(2, 2, R, L), vm(2, 6, G, R, L), vm(nz, 2, R, L), vm(nd, R, L),
                vm(X, R, L), vm(2, G, R, L), vm(R, L),
                vm(2, 2, R, L), vm(2, G, R, L), vm(nz, R, L), vm(nd, R, L),
                vm(2, G, R, L), vm(R, L),
                vm(2, 2, R, L), vm(2, G, R, L), vm(2, R, L),
                pltpu.SemaphoreType.DMA((2,)),
                pltpu.SemaphoreType.DMA((messages,)),
                pltpu.SemaphoreType.DMA((messages,)),
            ],
            compiler_params=pltpu.CompilerParams(collective_id=0, has_side_effects=True),
        )(conserved, sigma_guess)

    specs = (P(None, "gx", "gy", "gz"), P("gx", "gy", "gz"))
    return jax.shard_map(on_device, mesh=mesh, in_specs=specs, out_specs=specs, check_vma=False)
```

time: 90.8 us -> 25.1 us (0.28)
  waiting for transfers between devices: 48.7 us -> 0 us
  starting transfers between devices: 27.4 us -> 0 us
  Pallas kernels: 0 us -> 22.1 us
  other arithmetic: 8.34 us -> 0 us
  local copies, waits for them, and re-layouts: 4.71 us -> 2.22 us
    ppermute x30 -> x0, waiting for transfers between devices: 48.7 us -> none  [the longest x15 29 us: extended(): lax.ppermute(tail, axis, [(i, (i + 1) % count) for i in range(count)])]
    ppermute x30 -> x0, starting transfers between devices: 27.4 us -> none  [the longest x15 14.2 us: extended(): lax.ppermute(tail, axis, [(i, (i + 1) % count) for i in range(count)])]
    pallas_call x0 -> x1, Pallas kernels: none -> 22.1 us  [on_device(): pl.pallas_call(functools.partial(kernel, sizes), out_shape=(jax.ShapeDtyp...]
    concatenate x9 -> x0, other arithmetic: 2.25 us -> none  [extended(): jnp.concatenate([lax.ppermute(tail, axis, [(i, (i + 1) % count) for i in...]
    div x10 -> x0, other arithmetic: 2.18 us -> none  [the longest x4 0.75 us: jacobi_sweep(): return (ALPHA * source + ALPHA * acc_num) / (centre + ALPHA * acc_den)]
    slice x7 -> x0, other arithmetic: 2.11 us -> none  [the longest x6 1.96 us: extended(): lax.slice_in_dim(cells, cells.shape[dim] - width, cells.shape[dim], axis=...]
    ppermute x2 -> x0, local copies, waits for them, and re-layouts: 1.99 us -> none  [the longest x1 1.43 us: extended(): lax.ppermute(tail, axis, [(i, (i + 1) % count) for i in range(count)])]
    unnamed x13 -> x4, local copies, waits for them, and re-layouts: 1.75 us -> 2.22 us
  transfers between devices with their start and end apart: 30 -> 0, of which waited for: 28 -> 0; matrix products, arithmetic and copies ran while one was open for 5% -> 0% of each run, Pallas kernels for 0% -> 0%
where the time goes in v1:
time: 25.1 us; the launch traced here: 24.9 us
  Pallas kernels  22.1 us (88%)
  local copies, waits for them, and re-layouts  2.22 us (9%)
  between operations  0.65 us (3%)
    pallas_call x1, Pallas kernels, on_device(): pl.pallas_call(functools.partial(kernel, sizes), out_shape=(jax.ShapeDtyp...  22.1 us
    unnamed x4, local copies, waits for them, and re-layouts  2.22 us

profile of v1, /device:TPU:0, one launch (start us, length us, event | category | flops | bytes accessed | tf_op | source)
XLA Modules:
  0.0 24.9 jit_solution(7789664959690983569)
XLA Ops:
  0.6 22.1 %shard_map.41 = (f32[5,8,8,128]{3,2,1,0:T(8,128)}, f32[8,8,128]{2,1,0:T(8,128)}) custom-call(f32[5,8,8,128]{3,2,1,0:T(8,128)} %cons_hbm.1, f32[8,8,128]{2,1,0:T(8,128)} %sig_hbm.1), custom_call_target="tpu_custom_call" | custom-call | tf_op jit(solution)/shard_map/pallas_call | solution.py:350
  22.7 0.0 copy-start
  22.7 1.6 %copy.6 = f32[5,8,8,128]{3,2,1,0:T(8,128)} copy(f32[5,8,8,128]{3,2,1,0:T(8,128)} %get-tuple-element.4) | data formatting | bytes 327680
  24.3 0.0 copy-done
  24.3 0.6 %copy.7 = f32[8,8,128]{2,1,0:T(8,128)} copy(f32[8,8,128]{2,1,0:T(8,128)S(1)} %copy-done) | data formatting | bytes 65536
Async XLA Ops:
  22.7 1.6 %copy-start = (f32[8,8,128]{2,1,0:T(8,128)S(1)}, f32[8,8,128]{2,1,0:T(8,128)}, u32[]{:S(2)}) copy-start(f32[8,8,128]{2,1,0:T(8,128)} %get-tuple-element.5) | copy-start | bytes 98308

commit v2 on v1

--- a/solution.py
+++ b/solution.py
@@ -349,7 +349,7 @@
         messages = 48
         return pl.pallas_call(
             functools.partial(kernel, sizes),
-            out_shape=(jax.ShapeDtypeStruct(conserved.shape, f32), jax.ShapeDtypeStruct(sigma_guess.shape, f32)),
+            out_shape=(pltpu.VMEM(conserved.shape, f32), pltpu.VMEM(sigma_guess.shape, f32)),
             in_specs=[pl.BlockSpec(memory_space=pl.ANY)] * 2,
             out_specs=(pl.BlockSpec(memory_space=pltpu.VMEM),) * 2,
             scratch_shapes=[

time: 25.1 us -> 23.5 us (0.936)
  local copies, waits for them, and re-layouts: 2.22 us -> 1.28 us
  Pallas kernels: 22.1 us -> 21.4 us
    unnamed x4 -> x2, local copies, waits for them, and re-layouts: 2.22 us -> 1.28 us
    pallas_call x1, Pallas kernels: 22.1 us -> 21.4 us  [on_device(): pl.pallas_call(functools.partial(kernel, sizes), out_shape=(pltpu.VMEM(co...]
where the time goes in v2:
time: 23.5 us; the launch traced here: 23.3 us
  Pallas kernels  21.4 us (91%)
  local copies, waits for them, and re-layouts  1.28 us (5%)
  between operations  0.64 us (3%)
    pallas_call x1, Pallas kernels, on_device(): pl.pallas_call(functools.partial(kernel, sizes), out_shape=(pltpu.VMEM(co...  21.4 us
    unnamed x2, local copies, waits for them, and re-layouts  1.28 us

profile of v2, /device:TPU:0, one launch (start us, length us, event | category | flops | bytes accessed | tf_op | source)
XLA Modules:
  0.0 23.3 jit_solution(4331218764781506312)
XLA Ops:
  0.6 21.4 %shard_map.41 = (f32[5,8,8,128]{3,2,1,0:T(8,128)S(1)}, f32[8,8,128]{2,1,0:T(8,128)S(1)}) custom-call(f32[5,8,8,128]{3,2,1,0:T(8,128)} %cons_hbm.1, f32[8,8,128]{2,1,0:T(8,128)} %sig_hbm.1), custom_call_target="tpu_custom_call" | custom-call | tf_op jit(solution)/shard_map/pallas_call | solution.py:350
  22.1 0.7 %copy.6 = f32[5,8,8,128]{3,2,1,0:T(8,128)} copy(f32[5,8,8,128]{3,2,1,0:T(8,128)S(1)} %get-tuple-element.2) | data formatting | bytes 327680
  22.7 0.6 %copy.7 = f32[8,8,128]{2,1,0:T(8,128)} copy(f32[8,8,128]{2,1,0:T(8,128)S(1)} %get-tuple-element.3) | data formatting | bytes 65536

commit v3 on v2

v3 whole, which is shorter than its diff:
```python
import functools
import itertools

import jax
import jax.numpy as jnp
from jax import lax
from jax.experimental import pallas as pl
from jax.experimental.pallas import tpu as pltpu
from jax.sharding import PartitionSpec as P

SWEEPS = 4
ALPHA = 10.0
GAMMA = 1.4
LAMBDA = 3.0
STEP_DT = 0.4
MESH = pl.DeviceIdType.MESH
AXES = ("gx", "gy", "gz")

OFFSETS = [o for o in itertools.product((-1, 0, 1), repeat=3) if 1 <= sum(abs(v) for v in o) <= 2]
NEAR = [o for o in OFFSETS if sum(abs(v) for v in o) == 1]
Z_MOVES = [o for o in OFFSETS if o[2] != 0]
XY_MOVES = [o for o in OFFSETS if o[0] != 0 and o[1] != 0]


def neg(offset):
    return tuple(-v for v in offset)


def iota(shape, dim):
    return lax.broadcasted_iota(jnp.int32, shape, dim)


def roll(value, shift, axis):
    size = value.shape[axis]
    shift = shift % size
    return value if shift == 0 else pltpu.roll(value, shift, axis)


def ring(core, ghost, step, axis):
    size = core.shape[axis]
    a, b = roll(core, -step, axis), roll(ghost, -step, axis)
    edge = iota(core.shape, axis) == (size - 1 if step == 1 else 0)
    return jnp.where(edge, b, a), jnp.where(edge, a, b)


def kernel(sizes, cons_hbm, sig_hbm, adv_ref, out_sig_ref, cons, sig,
           yas, zas, xar, xsr, yar, zar,
           ybs, yrs, zrs, xbr, xer, xtr, ybr, yrr, zrr, drr,
           s1, src, y2s, z2s, x2r, x2q, y2r, z2r, d2r,
           s3, y3s, z3s, x3r, y3r, z3r, d3r,
           in_sem, send_sem, recv_sem):
    X, R, L = sig.shape
    me = [lax.axis_index(a) for a in AXES]

    def device(offset):
        return {a: lax.rem(me[i] + offset[i] + sizes[i], sizes[i]) for i, a in enumerate(AXES)}

    load_c = pltpu.make_async_copy(cons_hbm, cons, in_sem.at[0])
    load_s = pltpu.make_async_copy(sig_hbm, sig, in_sem.at[1])
    load_c.start()
    load_s.start()
    barrier = pltpu.get_barrier_semaphore()
    for o in NEAR:
        pl.semaphore_signal(barrier, inc=1, device_id=device(o), device_id_type=MESH)

    sent = []
    count = [0]

    def send(src, dst, offset):
        n = count[0]
        count[0] += 1
        copy = pltpu.make_async_remote_copy(
            src_ref=src, dst_ref=dst, send_sem=send_sem.at[n], recv_sem=recv_sem.at[n],
            device_id=device(offset), device_id_type=MESH)
        copy.start()
        sent.append(copy)
        return copy

    rows = lambda shape: iota(shape, len(shape) - 2)
    lanes = lambda shape: iota(shape, len(shape) - 1)

    def pack_rows(field, first, n):
        size = X * n // R
        out = field[0:size]
        r = rows(out.shape)
        for g in range(1, R // n):
            part = roll(field[g * size:(g + 1) * size], n * g, 1)
            out = jnp.where((r + (2 * R - first - n * g)) % R < n, part, out)
        return out

    def unpack_rows(after, before, n):
        low = rows(after.shape) < R // 2
        return jnp.concatenate(
            [jnp.where(low, roll(after, -n * g, 1), roll(before, -n * g, 1)) for g in range(R // n)], axis=0)

    lane2, row2 = lanes((R, L)), rows((R, L))

    def pack_lanes(fields, width):
        out = jnp.zeros((R, L), jnp.float32)
        for k, tile in enumerate(f[p] for f in fields for p in range(X)):
            out = jnp.where(((lane2 + width // 2) % L) // width == k, roll(tile, width * k, 1), out)
        return out

    def merge_lanes(after, before, width):
        return jnp.where(lanes(after.shape) % width < width // 2, after, before)

    def unpack_lanes(packed, ks, width):
        return jnp.concatenate([roll(packed, -width * k, 1)[None] for k in ks], axis=0)

    def cat(*parts):
        return jnp.concatenate(parts, axis=0)

    def wait(copies):
        for copy in copies:
            copy.wait_recv()

    ups = ((0, 1), (1, -1))

    def edge(d, count, back=0):
        return pl.ds(X - count - back, count) if d == 1 else pl.ds(back, count)

    def send_z(src_ref, dst_ref):
        return [send(src_ref, dst_ref.at[n], o) for n, o in enumerate(Z_MOVES)]

    def z_tiles(buf, e, width, f=0):
        def of(dx, dy):
            return merge_lanes(buf[Z_MOVES.index((-dx, -dy, -1))], buf[Z_MOVES.index((-dx, -dy, 1))], width)
        k = f * X
        z = cat(unpack_lanes(of(-1, 0), range(k + X - e, k + X), width),
                unpack_lanes(of(0, 0), range(k, k + X), width),
                unpack_lanes(of(1, 0), range(k, k + e), width))
        diag = jnp.where(row2 < R // 2, of(0, 1), of(0, -1))
        return z, unpack_lanes(diag, range(k, k + X), width)

    def corners(buf, dx):
        after, before = buf[XY_MOVES.index((-dx, -1, 0))], buf[XY_MOVES.index((-dx, 1, 0))]
        return jnp.where(rows(after.shape) < R // 2, after, before)

    load_c.wait()
    load_s.wait()
    pl.semaphore_wait(barrier, len(NEAR))
    got1 = []
    state = [cons[f] for f in range(4)] + [sig[...]]
    for f in range(5):
        yas[0, f] = pack_rows(state[f], R - 1, 1)
        yas[1, f] = pack_rows(state[f], 0, 1)
    for j, d in ups:
        got1.append(send(yas.at[j], yar.at[j], (0, d, 0)))
    for j, d in ups:
        got1.append(send(cons.at[0:4, edge(d, 1)], xar.at[j], (d, 0, 0)))
        got1.append(send(sig.at[edge(d, 1)], xsr.at[j], (d, 0, 0)))
    energy = cons[4]
    zas[0] = pack_lanes(state[0:4], 4)
    zas[1] = pack_lanes([state[4], energy], 4)
    for j, d in ups:
        got1.append(send(zas, zar.at[j], (0, 0, d)))

    late, late_rho = [], []
    for f in range(4):
        field = state[1 + f] if f < 3 else energy
        ybs[0, f] = pack_rows(field, R - 2, 2)
        ybs[1, f] = pack_rows(field, 0, 2)
    yrs[0] = pack_rows(state[0], R // 2, R // 2)
    yrs[1] = pack_rows(state[0], 0, R // 2)
    for j, d in ups:
        late.append(send(yrs.at[j], yrr.at[j], (0, d, 0)))
        late.append(send(ybs.at[j], ybr.at[j], (0, d, 0)))
        late.append(send(cons.at[0:5, edge(d, 1, 1)], xbr.at[j], (d, 0, 0)))
        late.append(send(cons.at[4, edge(d, 1)], xer.at[j], (d, 0, 0)))
        late_rho.append(send(cons.at[0, edge(d, 1, 2)], xtr.at[j], (d, 0, 0)))
    zrs[...] = pack_lanes([state[0]], 8)

    wait(got1)
    late_rho += [send(cons.at[0, edge(o[0], 2)], drr.at[n], o) for n, o in enumerate(XY_MOVES)]
    late_rho += send_z(zrs, zrr)

    zmerged = [merge_lanes(zar[1, v], zar[0, v], 4) for v in range(2)]

    def near(f):
        ghost_x = (xar[0, f], xar[1, f]) if f < 4 else (xsr[0], xsr[1])
        y = unpack_rows(yar[1, f], yar[0, f], 1)
        z = unpack_lanes(zmerged[f // 4], [(f % 4) * X + p for p in range(X)], 4)
        return cat(ghost_x[0], state[f], ghost_x[1]), y, z

    def neighbours(field):
        c, y, z = field
        m = c[1:X + 1]
        return [(c[2:X + 2], c[0:X]),
                (ring(m, y, 1, 1)[0], ring(m, y, -1, 1)[0]),
                (ring(m, z, 1, 2)[0], ring(m, z, -1, 2)[0])]

    def coefficients(inv_m, inv_n):
        ws = [[0.5 * (inv_m + inv_n[d][s]) for s in range(2)] for d in range(3)]
        return ws, ALPHA / (inv_m + ALPHA * sum(w for pair in ws for w in pair))

    def update(source, ws, scale, nbr):
        acc = source
        for d in range(3):
            for s in range(2):
                acc = acc + ws[d][s] * nbr[d][s]
        return acc * scale

    ext = [near(f) for f in range(5)]
    inv = tuple(1.0 / v for v in ext[0])
    g = []
    for k in (1, 2, 3):
        n = neighbours(tuple(m * r for m, r in zip(ext[k], inv)))
        g.append([0.5 * (n[d][0] - n[d][1]) for d in range(3)])
    div = g[0][0] + g[1][1] + g[2][2]
    source = (g[0][0] * g[0][0] + g[1][1] * g[1][1] + g[2][2] * g[2][2]
              + 2.0 * (g[0][1] * g[1][0] + g[0][2] * g[2][0] + g[1][2] * g[2][1]) + div * div)
    src[...] = source
    near_w, near_scale = coefficients(inv[0][1:X + 1], neighbours(inv))
    sigma1 = update(source, near_w, near_scale, neighbours(ext[4]))

    s1[...] = sigma1
    for j, first in ((0, R - 2), (1, 0)):
        y2s[j, 0] = pack_rows(sigma1, first, 2)
        y2s[j, 1] = pack_rows(source, first, 2)
    z2s[...] = pack_lanes([sigma1, source], 4)
    got2 = [send(s1.at[X - 1 if o[0] == 1 else 0], d2r.at[n], o) for n, o in enumerate(XY_MOVES)]
    got2 += send_z(z2s, z2r)
    for j, d in ups:
        got2.append(send(y2s.at[j], y2r.at[j], (0, d, 0)))
        got2.append(send(s1.at[edge(d, 2)], x2r.at[j], (d, 0, 0)))
        got2.append(send(src.at[edge(d, 2)], x2q.at[j], (d, 0, 0)))

    wait(late)
    core = state[0:4] + [energy]
    rho_y = unpack_rows(yrr[1], yrr[0], R // 2)
    xc = [cat(xbr[0, f], xar[0, f], core[f], xar[1, f], xbr[1, f]) for f in range(4)]
    xc.append(cat(xbr[0, 4], xer[0], energy, xer[1], xbr[1, 4]))
    yc = [rho_y] + [unpack_rows(ybr[1, f], ybr[0, f], 2) for f in range(4)]
    zc = [ext[f][2] for f in range(4)] + [unpack_lanes(zmerged[1], range(X, 2 * X), 4)]

    def x_stencil(c):
        return c[0:X + 1], c[1:X + 2], c[2:X + 3], c[3:X + 4]

    def ring_stencil(c, gh, axis):
        m, p = ring(c, gh, -1, axis), ring(c, gh, 1, axis)
        return cat(*m), cat(c, gh), cat(*p), cat(*ring(p[0], p[1], 1, axis))

    def faces(st):
        m, q, p, pp = st
        sixth = 1.0 / 6.0
        return (5.0 * q + 2.0 * p - m) * sixth, (2.0 * q + 5.0 * p - pp) * sixth

    def plain_flux(s, d):
        r = 1.0 / s[0]
        v = s[1 + d] * r
        pressure = (GAMMA - 1.0) * (s[4] - 0.5 * (s[1] * s[1] + s[2] * s[2] + s[3] * s[3]) * r)
        out = [s[1 + d]]
        for k in range(3):
            out.append(s[1 + k] * v + pressure if k == d else s[1 + k] * v)
        out.append((s[4] + pressure) * v)
        return out, v

    def difference(flux, d):
        if d == 0:
            return flux[1:X + 1] - flux[0:X]
        return flux[0:X] - ring(flux[0:X], flux[X:2 * X], -1, d)[0]

    base = [None] * 5
    speed = []
    for d in range(3):
        if d == 0:
            lr = [faces(x_stencil(c)) for c in xc]
        else:
            lr = [faces(ring_stencil(c, gh, d)) for c, gh in zip(core, (None, yc, zc)[d])]
        lf, lv = plain_flux([v[0] for v in lr], d)
        rf, rv = plain_flux([v[1] for v in lr], d)
        speed.append((lv, rv))
        for k in range(5):
            flux = 0.5 * (lf[k] + rf[k]) - (0.5 * LAMBDA) * (lr[k][1] - lr[k][0])
            change = difference(flux, d)
            base[k] = change if base[k] is None else base[k] + change
    base = [core[k] - STEP_DT * base[k] for k in range(5)]
    adv_ref[0] = base[0]

    def around(field, e):
        c, y, z, w = field
        size = X + 2 * e
        cm = c[1:size + 1]
        own = slice(e, e + X)
        yp, ym = ring(cm, y, 1, 1), ring(cm, y, -1, 1)
        zp, zm = ring(cm, z, 1, 2), ring(cm, z, -1, 2)
        zy = [ring(z[own], w, s, 1)[0] for s in (1, -1)]
        yz = [ring(y[own], w, s, 2)[0] for s in (1, -1)]
        xs = lambda t: (t[e + 1:e + X + 1], t[e - 1:e + X - 1])
        return ([(c[2:size + 2], c[0:size]), (yp[0], ym[0]), (zp[0], zm[0])],
                [xs(y), (yp[1][own], ym[1][own]), yz],
                [xs(z), zy, (zp[1][own], zm[1][own])])

    wait(late_rho)
    rho_c = cat(xtr[0], xc[0], xtr[1])
    rho_z, rho_w = z_tiles(zrr, 2, 8)
    inv = tuple(1.0 / v for v in (rho_c, cat(corners(drr, -1), rho_y, corners(drr, 1)), rho_z, rho_w))
    inv_n = around(inv, 2)
    inv_m = (inv[0][1:X + 5], inv[1][2:X + 2], inv[2][2:X + 2])
    coef = [coefficients(m, n) for m, n in zip(inv_m, inv_n)]

    wait(got2)
    z, w = z_tiles(z2r, 1, 4)
    field = (cat(x2r[0], sigma1, x2r[1]),
             cat(corners(d2r, -1)[None], unpack_rows(y2r[1, 0], y2r[0, 0], 2), corners(d2r, 1)[None]), z, w)
    zs = merge_lanes(z2r[Z_MOVES.index((0, 0, -1))], z2r[Z_MOVES.index((0, 0, 1))], 4)
    sources = (cat(x2q[0], source, x2q[1]), unpack_rows(y2r[1, 1], y2r[0, 1], 2),
               unpack_lanes(zs, range(X, 2 * X), 4))
    inner = slice(1, X + 3)
    n = around(field, 1)
    c = update(sources[0][inner], [[v[inner] for v in pair] for pair in coef[0][0]], coef[0][1][inner], n[0])
    y = update(sources[1], *coef[1], n[1])
    z = update(sources[2], *coef[2], n[2])
    sigma3 = update(source, near_w, near_scale, neighbours((c, y, z)))

    s3[...] = sigma3
    y3s[0] = pack_rows(sigma3, R // 2, R // 2)
    y3s[1] = pack_rows(sigma3, 0, R // 2)
    z3s[...] = pack_lanes([sigma3], 8)
    got3 = [send(s3.at[edge(o[0], 2)], d3r.at[k], o) for k, o in enumerate(XY_MOVES)]
    got3 += send_z(z3s, z3r)
    for j, d in ups:
        got3.append(send(y3s.at[j], y3r.at[j], (0, d, 0)))
        got3.append(send(s3.at[edge(d, 3)], x3r.at[j], (d, 0, 0)))
    wait(got3)

    z, w = z_tiles(z3r, 2, 8)
    field = (cat(x3r[0], sigma3, x3r[1]),
             cat(corners(d3r, -1), unpack_rows(y3r[1], y3r[0], R // 2), corners(d3r, 1)), z, w)
    n = around(field, 2)
    c, y, z = (update(sources[t], *coef[t], n[t]) for t in range(3))
    sigma4 = c[2:X + 2]
    out_sig_ref[...] = sigma4
    total = base[4]
    for d in range(3):
        ls, rs = faces(x_stencil(c) if d == 0 else ring_stencil(sigma4, y if d == 1 else z, d))
        lv, rv = speed[d]
        adv_ref[1 + d] = base[1 + d] - (0.5 * STEP_DT) * difference(ls + rs, d)
        total = total - (0.5 * STEP_DT) * difference(ls * lv + rs * rv, d)
    adv_ref[4] = total
    for copy in sent:
        copy.wait_send()


def solution(mesh):
    sizes = tuple(mesh.shape[a] for a in AXES)

    def on_device(conserved, sigma_guess):
        X, R, L = sigma_guess.shape
        A, B, H = X // R, 2 * X // R, X // 2
        f32 = jnp.float32
        vm = lambda *shape: pltpu.VMEM(shape, f32)
        nz, nd = len(Z_MOVES), len(XY_MOVES)
        messages = 80
        return pl.pallas_call(
            functools.partial(kernel, sizes),
            out_shape=(pltpu.VMEM(conserved.shape, f32), pltpu.VMEM(sigma_guess.shape, f32)),
            in_specs=[pl.BlockSpec(memory_space=pl.ANY)] * 2,
            out_specs=(pl.BlockSpec(memory_space=pltpu.VMEM),) * 2,
            scratch_shapes=[
                vm(*conserved.shape), vm(X, R, L),
                vm(2, 5, A, R, L), vm(2, R, L), vm(2, 4, 1, R, L), vm(2, 1, R, L), vm(2, 5, A, R, L), vm(2, 2, R, L),
                vm(2, 4, B, R, L), vm(2, H, R, L), vm(R, L), vm(2, 5, 1, R, L), vm(2, 1, R, L), vm(2, 1, R, L),
                vm(2, 4, B, R, L), vm(2, H, R, L), vm(nz, R, L), vm(nd, 2, R, L),
                vm(X, R, L), vm(X, R, L), vm(2, 2, B, R, L), vm(R, L),
                vm(2, 2, R, L), vm(2, 2, R, L), vm(2, 2, B, R, L), vm(nz, R, L), vm(nd, R, L),
                vm(X, R, L), vm(2, H, R, L), vm(R, L),
                vm(2, 3, R, L), vm(2, H, R, L), vm(nz, R, L), vm(nd, 2, R, L),
                pltpu.SemaphoreType.DMA((2,)),
                pltpu.SemaphoreType.DMA((messages,)),
                pltpu.SemaphoreType.DMA((messages,)),
            ],
            compiler_params=pltpu.CompilerParams(collective_id=0, has_side_effects=True),
        )(conserved, sigma_guess)

    specs = (P(None, "gx", "gy", "gz"), P("gx", "gy", "gz"))
    return jax.shard_map(on_device, mesh=mesh, in_specs=specs, out_specs=specs, check_vma=False)
```

time: 23.5 us -> 22.9 us (0.974)
  Pallas kernels: 21.4 us -> 20.9 us
    pallas_call x1, Pallas kernels: 21.4 us -> 20.9 us  [on_device(): pl.pallas_call(functools.partial(kernel, sizes), out_shape=(pltpu.VMEM(co...]
where the time goes in v3:
time: 22.9 us; the launch traced here: 22.8 us
  Pallas kernels  20.9 us (91%)
  local copies, waits for them, and re-layouts  1.28 us (6%)
  between operations  0.64 us (3%)
    pallas_call x1, Pallas kernels, on_device(): pl.pallas_call(functools.partial(kernel, sizes), out_shape=(pltpu.VMEM(co...  20.9 us
    unnamed x2, local copies, waits for them, and re-layouts  1.28 us

profile of v3, /device:TPU:0, one launch (start us, length us, event | category | flops | bytes accessed | tf_op | source)
XLA Modules:
  0.0 22.8 jit_solution(9630169368355717244)
XLA Ops:
  0.6 20.9 %shard_map.41 = (f32[5,8,8,128]{3,2,1,0:T(8,128)S(1)}, f32[8,8,128]{2,1,0:T(8,128)S(1)}) custom-call(f32[5,8,8,128]{3,2,1,0:T(8,128)} %cons_hbm.1, f32[8,8,128]{2,1,0:T(8,128)} %sig_hbm.1), custom_call_target="tpu_custom_call" | custom-call | tf_op jit(solution)/shard_map/pallas_call | solution.py:355
  21.5 0.7 %copy.6 = f32[5,8,8,128]{3,2,1,0:T(8,128)} copy(f32[5,8,8,128]{3,2,1,0:T(8,128)S(1)} %get-tuple-element.2) | data formatting | bytes 327680
  22.2 0.6 %copy.7 = f32[8,8,128]{2,1,0:T(8,128)} copy(f32[8,8,128]{2,1,0:T(8,128)S(1)} %get-tuple-element.3) | data formatting | bytes 65536

commit v4 on v3

--- a/solution.py
+++ b/solution.py
@@ -155,19 +155,12 @@
     for j, d in ups:
         got1.append(send(zas, zar.at[j], (0, 0, d)))
 
-    late, late_rho = [], []
-    for f in range(4):
-        field = state[1 + f] if f < 3 else energy
-        ybs[0, f] = pack_rows(field, R - 2, 2)
-        ybs[1, f] = pack_rows(field, 0, 2)
+    late_rho = []
     yrs[0] = pack_rows(state[0], R // 2, R // 2)
     yrs[1] = pack_rows(state[0], 0, R // 2)
     for j, d in ups:
-        late.append(send(yrs.at[j], yrr.at[j], (0, d, 0)))
-        late.append(send(ybs.at[j], ybr.at[j], (0, d, 0)))
-        late.append(send(cons.at[0:5, edge(d, 1, 1)], xbr.at[j], (d, 0, 0)))
-        late.append(send(cons.at[4, edge(d, 1)], xer.at[j], (d, 0, 0)))
-        late_rho.append(send(cons.at[0, edge(d, 1, 2)], xtr.at[j], (d, 0, 0)))
+        late_rho.append(send(yrs.at[j], yrr.at[j], (0, d, 0)))
+        late_rho.append(send(cons.at[0, edge(d, 2, 1)], xtr.at[j], (d, 0, 0)))
     zrs[...] = pack_lanes([state[0]], 8)
 
     wait(got1)
@@ -225,11 +218,65 @@
         got2.append(send(s1.at[edge(d, 2)], x2r.at[j], (d, 0, 0)))
         got2.append(send(src.at[edge(d, 2)], x2q.at[j], (d, 0, 0)))
 
+    late = []
+    for f in range(4):
+        part = state[1 + f] if f < 3 else energy
+        ybs[0, f] = pack_rows(part, R - 2, 2)
+        ybs[1, f] = pack_rows(part, 0, 2)
+    for j, d in ups:
+        late.append(send(ybs.at[j], ybr.at[j], (0, d, 0)))
+        late.append(send(cons.at[1:5, edge(d, 1, 1)], xbr.at[j], (d, 0, 0)))
+        late.append(send(cons.at[4, edge(d, 1)], xer.at[j], (d, 0, 0)))
+    def around(field, e):
+        c, y, z, w = field
+        size = X + 2 * e
+        cm = c[1:size + 1]
+        own = slice(e, e + X)
+        yp, ym = ring(cm, y, 1, 1), ring(cm, y, -1, 1)
+        zp, zm = ring(cm, z, 1, 2), ring(cm, z, -1, 2)
+        zy = [ring(z[own], w, s, 1)[0] for s in (1, -1)]
+        yz = [ring(y[own], w, s, 2)[0] for s in (1, -1)]
+        xs = lambda t: (t[e + 1:e + X + 1], t[e - 1:e + X - 1])
+        return ([(c[2:size + 2], c[0:size]), (yp[0], ym[0]), (zp[0], zm[0])],
+                [xs(y), (yp[1][own], ym[1][own]), yz],
+                [xs(z), zy, (zp[1][own], zm[1][own])])
+
+    wait(late_rho)
+    rho_y = unpack_rows(yrr[1], yrr[0], R // 2)
+    rho_c = cat(xtr[0], xar[0, 0], state[0], xar[1, 0], xtr[1])
+    rho_z, rho_w = z_tiles(zrr, 2, 8)
+    inv = tuple(1.0 / v for v in (rho_c, cat(corners(drr, -1), rho_y, corners(drr, 1)), rho_z, rho_w))
+    inv_n = around(inv, 2)
+    inv_m = (inv[0][1:X + 5], inv[1][2:X + 2], inv[2][2:X + 2])
+    coef = [coefficients(m, n) for m, n in zip(inv_m, inv_n)]
+
+    wait(got2)
+    z, w = z_tiles(z2r, 1, 4)
+    field = (cat(x2r[0], sigma1, x2r[1]),
+             cat(corners(d2r, -1)[None], unpack_rows(y2r[1, 0], y2r[0, 0], 2), corners(d2r, 1)[None]), z, w)
+    zs = merge_lanes(z2r[Z_MOVES.index((0, 0, -1))], z2r[Z_MOVES.index((0, 0, 1))], 4)
+    sources = (cat(x2q[0], source, x2q[1]), unpack_rows(y2r[1, 1], y2r[0, 1], 2),
+               unpack_lanes(zs, range(X, 2 * X), 4))
+    inner = slice(1, X + 3)
+    n = around(field, 1)
+    c = update(sources[0][inner], [[v[inner] for v in pair] for pair in coef[0][0]], coef[0][1][inner], n[0])
+    y = update(sources[1], *coef[1], n[1])
+    z = update(sources[2], *coef[2], n[2])
+    sigma3 = update(source, near_w, near_scale, neighbours((c, y, z)))
+
+    s3[...] = sigma3
+    y3s[0] = pack_rows(sigma3, R // 2, R // 2)
+    y3s[1] = pack_rows(sigma3, 0, R // 2)
+    z3s[...] = pack_lanes([sigma3], 8)
+    got3 = [send(s3.at[edge(o[0], 2)], d3r.at[k], o) for k, o in enumerate(XY_MOVES)]
+    got3 += send_z(z3s, z3r)
+    for j, d in ups:
+        got3.append(send(y3s.at[j], y3r.at[j], (0, d, 0)))
+        got3.append(send(s3.at[edge(d, 3)], x3r.at[j], (d, 0, 0)))
     wait(late)
     core = state[0:4] + [energy]
-    rho_y = unpack_rows(yrr[1], yrr[0], R // 2)
-    xc = [cat(xbr[0, f], xar[0, f], core[f], xar[1, f], xbr[1, f]) for f in range(4)]
-    xc.append(cat(xbr[0, 4], xer[0], energy, xer[1], xbr[1, 4]))
+    xc = [rho_c[1:X + 5]] + [cat(xbr[0, f - 1], xar[0, f], core[f], xar[1, f], xbr[1, f - 1]) for f in (1, 2, 3)]
+    xc.append(cat(xbr[0, 3], xer[0], energy, xer[1], xbr[1, 3]))
     yc = [rho_y] + [unpack_rows(ybr[1, f], ybr[0, f], 2) for f in range(4)]
     zc = [ext[f][2] for f in range(4)] + [unpack_lanes(zmerged[1], range(X, 2 * X), 4)]
 
@@ -277,51 +324,6 @@
     base = [core[k] - STEP_DT * base[k] for k in range(5)]
     adv_ref[0] = base[0]
 
-    def around(field, e):
-        c, y, z, w = field
-        size = X + 2 * e
-        cm = c[1:size + 1]
-        own = slice(e, e + X)
-        yp, ym = ring(cm, y, 1, 1), ring(cm, y, -1, 1)
-        zp, zm = ring(cm, z, 1, 2), ring(cm, z, -1, 2)
-        zy = [ring(z[own], w, s, 1)[0] for s in (1, -1)]
-        yz = [ring(y[own], w, s, 2)[0] for s in (1, -1)]
-        xs = lambda t: (t[e + 1:e + X + 1], t[e - 1:e + X - 1])
-        return ([(c[2:size + 2], c[0:size]), (yp[0], ym[0]), (zp[0], zm[0])],
-                [xs(y), (yp[1][own], ym[1][own]), yz],
-                [xs(z), zy, (zp[1][own], zm[1][own])])
-
-    wait(late_rho)
-    rho_c = cat(xtr[0], xc[0], xtr[1])
-    rho_z, rho_w = z_tiles(zrr, 2, 8)
-    inv = tuple(1.0 / v for v in (rho_c, cat(corners(drr, -1), rho_y, corners(drr, 1)), rho_z, rho_w))
-    inv_n = around(inv, 2)
-    inv_m = (inv[0][1:X + 5], inv[1][2:X + 2], inv[2][2:X + 2])
-    coef = [coefficients(m, n) for m, n in zip(inv_m, inv_n)]
-
-    wait(got2)
-    z, w = z_tiles(z2r, 1, 4)
-    field = (cat(x2r[0], sigma1, x2r[1]),
-             cat(corners(d2r, -1)[None], unpack_rows(y2r[1, 0], y2r[0, 0], 2), corners(d2r, 1)[None]), z, w)
-    zs = merge_lanes(z2r[Z_MOVES.index((0, 0, -1))], z2r[Z_MOVES.index((0, 0, 1))], 4)
-    sources = (cat(x2q[0], source, x2q[1]), unpack_rows(y2r[1, 1], y2r[0, 1], 2),
-               unpack_lanes(zs, range(X, 2 * X), 4))
-    inner = slice(1, X + 3)
-    n = around(field, 1)
-    c = update(sources[0][inner], [[v[inner] for v in pair] for pair in coef[0][0]], coef[0][1][inner], n[0])
-    y = update(sources[1], *coef[1], n[1])
-    z = update(sources[2], *coef[2], n[2])
-    sigma3 = update(source, near_w, near_scale, neighbours((c, y, z)))
-
-    s3[...] = sigma3
-    y3s[0] = pack_rows(sigma3, R // 2, R // 2)
-    y3s[1] = pack_rows(sigma3, 0, R // 2)
-    z3s[...] = pack_lanes([sigma3], 8)
-    got3 = [send(s3.at[edge(o[0], 2)], d3r.at[k], o) for k, o in enumerate(XY_MOVES)]
-    got3 += send_z(z3s, z3r)
-    for j, d in ups:
-        got3.append(send(y3s.at[j], y3r.at[j], (0, d, 0)))
-        got3.append(send(s3.at[edge(d, 3)], x3r.at[j], (d, 0, 0)))
     wait(got3)
 
     z, w = z_tiles(z3r, 2, 8)
@@ -360,7 +362,7 @@
             scratch_shapes=[
                 vm(*conserved.shape), vm(X, R, L),
                 vm(2, 5, A, R, L), vm(2, R, L), vm(2, 4, 1, R, L), vm(2, 1, R, L), vm(2, 5, A, R, L), vm(2, 2, R, L),
-                vm(2, 4, B, R, L), vm(2, H, R, L), vm(R, L), vm(2, 5, 1, R, L), vm(2, 1, R, L), vm(2, 1, R, L),
+                vm(2, 4, B, R, L), vm(2, H, R, L), vm(R, L), vm(2, 4, 1, R, L), vm(2, 1, R, L), vm(2, 2, R, L),
                 vm(2, 4, B, R, L), vm(2, H, R, L), vm(nz, R, L), vm(nd, 2, R, L),
                 vm(X, R, L), vm(X, R, L), vm(2, 2, B, R, L), vm(R, L),
                 vm(2, 2, R, L), vm(2, 2, R, L), vm(2, 2, B, R, L), vm(nz, R, L), vm(nd, R, L),

time: 22.9 us -> 23.2 us (1.013)
    pallas_call x1, Pallas kernels: 20.9 us -> 21.1 us  [on_device(): pl.pallas_call(functools.partial(kernel, sizes), out_shape=(pltpu.VMEM(co...]
where the time goes in v4:
time: 23.2 us; the launch traced here: 23.1 us
  Pallas kernels  21.1 us (91%)
  local copies, waits for them, and re-layouts  1.28 us (6%)
  between operations  0.64 us (3%)
    pallas_call x1, Pallas kernels, on_device(): pl.pallas_call(functools.partial(kernel, sizes), out_shape=(pltpu.VMEM(co...  21.1 us
    unnamed x2, local copies, waits for them, and re-layouts  1.28 us

profile of v4, /device:TPU:0, one launch (start us, length us, event | category | flops | bytes accessed | tf_op | source)
XLA Modules:
  0.0 23.1 jit_solution(9051359351284710819)
XLA Ops:
  0.6 21.1 %shard_map.41 = (f32[5,8,8,128]{3,2,1,0:T(8,128)S(1)}, f32[8,8,128]{2,1,0:T(8,128)S(1)}) custom-call(f32[5,8,8,128]{3,2,1,0:T(8,128)} %cons_hbm.1, f32[8,8,128]{2,1,0:T(8,128)} %sig_hbm.1), custom_call_target="tpu_custom_call" | custom-call | tf_op jit(solution)/shard_map/pallas_call | solution.py:357
  21.8 0.7 %copy.6 = f32[5,8,8,128]{3,2,1,0:T(8,128)} copy(f32[5,8,8,128]{3,2,1,0:T(8,128)S(1)} %get-tuple-element.2) | data formatting | bytes 327680
  22.4 0.6 %copy.7 = f32[8,8,128]{2,1,0:T(8,128)} copy(f32[8,8,128]{2,1,0:T(8,128)S(1)} %get-tuple-element.3) | data formatting | bytes 65536

commit v5 on v4

--- a/solution.py
+++ b/solution.py
@@ -120,7 +120,14 @@
         return pl.ds(X - count - back, count) if d == 1 else pl.ds(back, count)
 
     def send_z(src_ref, dst_ref):
-        return [send(src_ref, dst_ref.at[n], o) for n, o in enumerate(Z_MOVES)]
+        far = [n for n, o in enumerate(Z_MOVES) if o[1]] + [n for n, o in enumerate(Z_MOVES) if o[0]]
+        face = [n for n, o in enumerate(Z_MOVES) if o in NEAR]
+        return ([send(src_ref, dst_ref.at[n], Z_MOVES[n]) for n in far],
+                [send(src_ref, dst_ref.at[n], Z_MOVES[n]) for n in face])
+
+    def z_face(buf, width, f=0):
+        merged = merge_lanes(buf[Z_MOVES.index((0, 0, -1))], buf[Z_MOVES.index((0, 0, 1))], width)
+        return unpack_lanes(merged, range(f * X, f * X + X), width)
 
     def z_tiles(buf, e, width, f=0):
         def of(dx, dy):
@@ -165,7 +172,7 @@
 
     wait(got1)
     late_rho += [send(cons.at[0, edge(o[0], 2)], drr.at[n], o) for n, o in enumerate(XY_MOVES)]
-    late_rho += send_z(zrs, zrr)
+    late_rho += sum(send_z(zrs, zrr), [])
 
     zmerged = [merge_lanes(zar[1, v], zar[0, v], 4) for v in range(2)]
 
@@ -207,16 +214,17 @@
     sigma1 = update(source, near_w, near_scale, neighbours(ext[4]))
 
     s1[...] = sigma1
+    far2 = [send(s1.at[X - 1 if o[0] == 1 else 0], d2r.at[n], o) for n, o in enumerate(XY_MOVES)]
+    z2s[...] = pack_lanes([sigma1, source], 4)
+    far, face2 = send_z(z2s, z2r)
+    far2 += far
     for j, first in ((0, R - 2), (1, 0)):
         y2s[j, 0] = pack_rows(sigma1, first, 2)
         y2s[j, 1] = pack_rows(source, first, 2)
-    z2s[...] = pack_lanes([sigma1, source], 4)
-    got2 = [send(s1.at[X - 1 if o[0] == 1 else 0], d2r.at[n], o) for n, o in enumerate(XY_MOVES)]
-    got2 += send_z(z2s, z2r)
-    for j, d in ups:
-        got2.append(send(y2s.at[j], y2r.at[j], (0, d, 0)))
-        got2.append(send(s1.at[edge(d, 2)], x2r.at[j], (d, 0, 0)))
-        got2.append(send(src.at[edge(d, 2)], x2q.at[j], (d, 0, 0)))
+    for j, d in ups:
+        face2.append(send(y2s.at[j], y2r.at[j], (0, d, 0)))
+        face2.append(send(s1.at[edge(d, 2)], x2r.at[j], (d, 0, 0)))
+        face2.append(send(src.at[edge(d, 2)], x2q.at[j], (d, 0, 0)))
 
     late = []
     for f in range(4):
@@ -229,50 +237,48 @@
         late.append(send(cons.at[4, edge(d, 1)], xer.at[j], (d, 0, 0)))
     def around(field, e):
         c, y, z, w = field
-        size = X + 2 * e
-        cm = c[1:size + 1]
         own = slice(e, e + X)
-        yp, ym = ring(cm, y, 1, 1), ring(cm, y, -1, 1)
-        zp, zm = ring(cm, z, 1, 2), ring(cm, z, -1, 2)
-        zy = [ring(z[own], w, s, 1)[0] for s in (1, -1)]
-        yz = [ring(y[own], w, s, 2)[0] for s in (1, -1)]
+        sides = lambda t, at: cat(t[at:at + e], t[X + e + at:X + 2 * e + at])
+        core, cg, yg, zg = c[e + 1:e + X + 1], sides(c, 1), sides(y, 0), sides(z, 0)
+        both = lambda a, b, axis, part: [ring(a, b, s, axis)[part] for s in (1, -1)]
         xs = lambda t: (t[e + 1:e + X + 1], t[e - 1:e + X - 1])
-        return ([(c[2:size + 2], c[0:size]), (yp[0], ym[0]), (zp[0], zm[0])],
-                [xs(y), (yp[1][own], ym[1][own]), yz],
-                [xs(z), zy, (zp[1][own], zm[1][own])])
+        return ([(sides(c, 2), sides(c, 0)), both(cg, yg, 1, 0), both(cg, zg, 2, 0)],
+                [xs(y), both(core, y[own], 1, 1), both(y[own], w, 2, 0)],
+                [xs(z), both(z[own], w, 1, 0), both(core, z[own], 2, 1)])
 
     wait(late_rho)
     rho_y = unpack_rows(yrr[1], yrr[0], R // 2)
     rho_c = cat(xtr[0], xar[0, 0], state[0], xar[1, 0], xtr[1])
     rho_z, rho_w = z_tiles(zrr, 2, 8)
     inv = tuple(1.0 / v for v in (rho_c, cat(corners(drr, -1), rho_y, corners(drr, 1)), rho_z, rho_w))
-    inv_n = around(inv, 2)
-    inv_m = (inv[0][1:X + 5], inv[1][2:X + 2], inv[2][2:X + 2])
-    coef = [coefficients(m, n) for m, n in zip(inv_m, inv_n)]
-
-    wait(got2)
+    inv_m = (cat(inv[0][1:3], inv[0][X + 3:X + 5]), inv[1][2:X + 2], inv[2][2:X + 2])
+    coef = [coefficients(m, n) for m, n in zip(inv_m, around(inv, 2))]
+
+    wait(face2)
+    y = unpack_rows(y2r[1, 0], y2r[0, 0], 2)
+    z = z_face(z2r, 4)
+    sources = (cat(x2q[0], x2q[1]), unpack_rows(y2r[1, 1], y2r[0, 1], 2), z_face(z2r, 4, 1))
+    c = cat(x2r[0], sigma1, x2r[1])
+    sigma2 = update(source, near_w, near_scale, neighbours((c[1:X + 3], y, z)))
+    wait(far2)
     z, w = z_tiles(z2r, 1, 4)
-    field = (cat(x2r[0], sigma1, x2r[1]),
-             cat(corners(d2r, -1)[None], unpack_rows(y2r[1, 0], y2r[0, 0], 2), corners(d2r, 1)[None]), z, w)
-    zs = merge_lanes(z2r[Z_MOVES.index((0, 0, -1))], z2r[Z_MOVES.index((0, 0, 1))], 4)
-    sources = (cat(x2q[0], source, x2q[1]), unpack_rows(y2r[1, 1], y2r[0, 1], 2),
-               unpack_lanes(zs, range(X, 2 * X), 4))
-    inner = slice(1, X + 3)
-    n = around(field, 1)
-    c = update(sources[0][inner], [[v[inner] for v in pair] for pair in coef[0][0]], coef[0][1][inner], n[0])
+    n = around((c, cat(corners(d2r, -1)[None], y, corners(d2r, 1)[None]), z, w), 1)
+    mid = slice(1, 3)
+    cg = update(sources[0][mid], [[v[mid] for v in pair] for pair in coef[0][0]], coef[0][1][mid], n[0])
     y = update(sources[1], *coef[1], n[1])
     z = update(sources[2], *coef[2], n[2])
-    sigma3 = update(source, near_w, near_scale, neighbours((c, y, z)))
+    sigma3 = update(source, near_w, near_scale, neighbours((cat(cg[0:1], sigma2, cg[1:2]), y, z)))
 
     s3[...] = sigma3
+    far3 = [send(s3.at[edge(o[0], 2)], d3r.at[k], o) for k, o in enumerate(XY_MOVES)]
+    z3s[...] = pack_lanes([sigma3], 8)
+    far, face3 = send_z(z3s, z3r)
+    far3 += far
     y3s[0] = pack_rows(sigma3, R // 2, R // 2)
     y3s[1] = pack_rows(sigma3, 0, R // 2)
-    z3s[...] = pack_lanes([sigma3], 8)
-    got3 = [send(s3.at[edge(o[0], 2)], d3r.at[k], o) for k, o in enumerate(XY_MOVES)]
-    got3 += send_z(z3s, z3r)
-    for j, d in ups:
-        got3.append(send(y3s.at[j], y3r.at[j], (0, d, 0)))
-        got3.append(send(s3.at[edge(d, 3)], x3r.at[j], (d, 0, 0)))
+    for j, d in ups:
+        face3.append(send(y3s.at[j], y3r.at[j], (0, d, 0)))
+        face3.append(send(s3.at[edge(d, 3)], x3r.at[j], (d, 0, 0)))
     wait(late)
     core = state[0:4] + [energy]
     xc = [rho_c[1:X + 5]] + [cat(xbr[0, f - 1], xar[0, f], core[f], xar[1, f], xbr[1, f - 1]) for f in (1, 2, 3)]
@@ -324,15 +330,17 @@
     base = [core[k] - STEP_DT * base[k] for k in range(5)]
     adv_ref[0] = base[0]
 
-    wait(got3)
-
+
+    wait(face3)
+    y = unpack_rows(y3r[1], y3r[0], R // 2)
+    c = cat(x3r[0], sigma3, x3r[1])
+    sigma4 = update(source, near_w, near_scale, neighbours((c[2:X + 4], y, z_face(z3r, 8))))
+    out_sig_ref[...] = sigma4
+    wait(far3)
     z, w = z_tiles(z3r, 2, 8)
-    field = (cat(x3r[0], sigma3, x3r[1]),
-             cat(corners(d3r, -1), unpack_rows(y3r[1], y3r[0], R // 2), corners(d3r, 1)), z, w)
-    n = around(field, 2)
-    c, y, z = (update(sources[t], *coef[t], n[t]) for t in range(3))
-    sigma4 = c[2:X + 2]
-    out_sig_ref[...] = sigma4
+    n = around((c, cat(corners(d3r, -1), y, corners(d3r, 1)), z, w), 2)
+    cg, y, z = (update(sources[t], *coef[t], n[t]) for t in range(3))
+    c = cat(cg[0:2], sigma4, cg[2:4])
     total = base[4]
     for d in range(3):
         ls, rs = faces(x_stencil(c) if d == 0 else ring_stencil(sigma4, y if d == 1 else z, d))

time: 23.2 us -> 23.3 us (level)
  no operation moved by 1% of the time
where the time goes in v5:
time: 23.3 us; the launch traced here: 23.1 us
  Pallas kernels  21.2 us (91%)
  local copies, waits for them, and re-layouts  1.28 us (5%)
  between operations  0.64 us (3%)
    pallas_call x1, Pallas kernels, on_device(): pl.pallas_call(functools.partial(kernel, sizes), out_shape=(pltpu.VMEM(co...  21.2 us
    unnamed x2, local copies, waits for them, and re-layouts  1.28 us

profile of v5, /device:TPU:0, one launch (start us, length us, event | category | flops | bytes accessed | tf_op | source)
XLA Modules:
  0.0 23.1 jit_solution(14800445511319694749)
XLA Ops:
  0.6 21.2 %shard_map.41 = (f32[5,8,8,128]{3,2,1,0:T(8,128)S(1)}, f32[8,8,128]{2,1,0:T(8,128)S(1)}) custom-call(f32[5,8,8,128]{3,2,1,0:T(8,128)} %cons_hbm.1, f32[8,8,128]{2,1,0:T(8,128)} %sig_hbm.1), custom_call_target="tpu_custom_call" | custom-call | tf_op jit(solution)/shard_map/pallas_call | solution.py:365
  21.8 0.7 %copy.6 = f32[5,8,8,128]{3,2,1,0:T(8,128)} copy(f32[5,8,8,128]{3,2,1,0:T(8,128)S(1)} %get-tuple-element.2) | data formatting | bytes 327680
  22.5 0.6 %copy.7 = f32[8,8,128]{2,1,0:T(8,128)} copy(f32[8,8,128]{2,1,0:T(8,128)S(1)} %get-tuple-element.3) | data formatting | bytes 65536

commit v6 on v5

--- a/solution.py
+++ b/solution.py
@@ -45,8 +45,8 @@
 
 def kernel(sizes, cons_hbm, sig_hbm, adv_ref, out_sig_ref, cons, sig,
            yas, zas, xar, xsr, yar, zar,
-           ybs, yrs, zrs, xbr, xer, xtr, ybr, yrr, zrr, drr,
-           s1, src, y2s, z2s, x2r, x2q, y2r, z2r, d2r,
+           ybs, yrs, xbr, xer, xtr, ybr, yrr,
+           s1, src, y2s, z2s, d2s, x2r, x2q, y2r, z2r, d2r,
            s3, y3s, z3s, x3r, y3r, z3r, d3r,
            in_sem, send_sem, recv_sem):
     X, R, L = sig.shape
@@ -168,12 +168,11 @@
     for j, d in ups:
         late_rho.append(send(yrs.at[j], yrr.at[j], (0, d, 0)))
         late_rho.append(send(cons.at[0, edge(d, 2, 1)], xtr.at[j], (d, 0, 0)))
-    zrs[...] = pack_lanes([state[0]], 8)
+    z2s[1] = pack_lanes([state[0]], 8)
+    d2s[0, 1:3] = state[0][X - 2:X]
+    d2s[1, 1:3] = state[0][0:2]
 
     wait(got1)
-    late_rho += [send(cons.at[0, edge(o[0], 2)], drr.at[n], o) for n, o in enumerate(XY_MOVES)]
-    late_rho += sum(send_z(zrs, zrr), [])
-
     zmerged = [merge_lanes(zar[1, v], zar[0, v], 4) for v in range(2)]
 
     def near(f):
@@ -214,8 +213,10 @@
     sigma1 = update(source, near_w, near_scale, neighbours(ext[4]))
 
     s1[...] = sigma1
-    far2 = [send(s1.at[X - 1 if o[0] == 1 else 0], d2r.at[n], o) for n, o in enumerate(XY_MOVES)]
-    z2s[...] = pack_lanes([sigma1, source], 4)
+    d2s[0, 0] = sigma1[X - 1]
+    d2s[1, 0] = sigma1[0]
+    far2 = [send(d2s.at[0 if o[0] == 1 else 1], d2r.at[n], o) for n, o in enumerate(XY_MOVES)]
+    z2s[0] = pack_lanes([sigma1, source], 4)
     far, face2 = send_z(z2s, z2r)
     far2 += far
     for j, first in ((0, R - 2), (1, 0)):
@@ -246,23 +247,25 @@
                 [xs(y), both(core, y[own], 1, 1), both(y[own], w, 2, 0)],
                 [xs(z), both(z[own], w, 1, 0), both(core, z[own], 2, 1)])
 
-    wait(late_rho)
-    rho_y = unpack_rows(yrr[1], yrr[0], R // 2)
-    rho_c = cat(xtr[0], xar[0, 0], state[0], xar[1, 0], xtr[1])
-    rho_z, rho_w = z_tiles(zrr, 2, 8)
-    inv = tuple(1.0 / v for v in (rho_c, cat(corners(drr, -1), rho_y, corners(drr, 1)), rho_z, rho_w))
-    inv_m = (cat(inv[0][1:3], inv[0][X + 3:X + 5]), inv[1][2:X + 2], inv[2][2:X + 2])
-    coef = [coefficients(m, n) for m, n in zip(inv_m, around(inv, 2))]
-
-    wait(face2)
+    wait(late_rho + face2)
+    z_near = [z2r[n, 0] if o in NEAR else None for n, o in enumerate(Z_MOVES)]
     y = unpack_rows(y2r[1, 0], y2r[0, 0], 2)
-    z = z_face(z2r, 4)
-    sources = (cat(x2q[0], x2q[1]), unpack_rows(y2r[1, 1], y2r[0, 1], 2), z_face(z2r, 4, 1))
+    z = z_face(z_near, 4)
+    sources = (cat(x2q[0], x2q[1]), unpack_rows(y2r[1, 1], y2r[0, 1], 2), z_face(z_near, 4, 1))
     c = cat(x2r[0], sigma1, x2r[1])
     sigma2 = update(source, near_w, near_scale, neighbours((c[1:X + 3], y, z)))
     wait(far2)
-    z, w = z_tiles(z2r, 1, 4)
-    n = around((c, cat(corners(d2r, -1)[None], y, corners(d2r, 1)[None]), z, w), 1)
+    d_rho = [d2r[n, 1:3] for n in range(len(XY_MOVES))]
+    d_sig = [d2r[n, 0] for n in range(len(XY_MOVES))]
+    rho_y = unpack_rows(yrr[1], yrr[0], R // 2)
+    rho_c = cat(xtr[0], xar[0, 0], state[0], xar[1, 0], xtr[1])
+    rho_z, rho_w = z_tiles([z2r[n, 1] for n in range(len(Z_MOVES))], 2, 8)
+    inv = tuple(1.0 / v for v in (rho_c, cat(corners(d_rho, -1), rho_y, corners(d_rho, 1)), rho_z, rho_w))
+    inv_m = (cat(inv[0][1:3], inv[0][X + 3:X + 5]), inv[1][2:X + 2], inv[2][2:X + 2])
+    coef = [coefficients(m, n) for m, n in zip(inv_m, around(inv, 2))]
+
+    z, w = z_tiles([z2r[n, 0] for n in range(len(Z_MOVES))], 1, 4)
+    n = around((c, cat(corners(d_sig, -1)[None], y, corners(d_sig, 1)[None]), z, w), 1)
     mid = slice(1, 3)
     cg = update(sources[0][mid], [[v[mid] for v in pair] for pair in coef[0][0]], coef[0][1][mid], n[0])
     y = update(sources[1], *coef[1], n[1])
@@ -370,10 +373,10 @@
             scratch_shapes=[
                 vm(*conserved.shape), vm(X, R, L),
                 vm(2, 5, A, R, L), vm(2, R, L), vm(2, 4, 1, R, L), vm(2, 1, R, L), vm(2, 5, A, R, L), vm(2, 2, R, L),
-                vm(2, 4, B, R, L), vm(2, H, R, L), vm(R, L), vm(2, 4, 1, R, L), vm(2, 1, R, L), vm(2, 2, R, L),
-                vm(2, 4, B, R, L), vm(2, H, R, L), vm(nz, R, L), vm(nd, 2, R, L),
-                vm(X, R, L), vm(X, R, L), vm(2, 2, B, R, L), vm(R, L),
-                vm(2, 2, R, L), vm(2, 2, R, L), vm(2, 2, B, R, L), vm(nz, R, L), vm(nd, R, L),
+                vm(2, 4, B, R, L), vm(2, H, R, L), vm(2, 4, 1, R, L), vm(2, 1, R, L), vm(2, 2, R, L),
+                vm(2, 4, B, R, L), vm(2, H, R, L),
+                vm(X, R, L), vm(X, R, L), vm(2, 2, B, R, L), vm(2, R, L), vm(2, 3, R, L),
+                vm(2, 2, R, L), vm(2, 2, R, L), vm(2, 2, B, R, L), vm(nz, 2, R, L), vm(nd, 3, R, L),
                 vm(X, R, L), vm(2, H, R, L), vm(R, L),
                 vm(2, 3, R, L), vm(2, H, R, L), vm(nz, R, L), vm(nd, 2, R, L),
                 pltpu.SemaphoreType.DMA((2,)),

time: 23.3 us -> 23.6 us (1.013)
  Pallas kernels: 21.2 us -> 21.6 us
    pallas_call x1, Pallas kernels: 21.2 us -> 21.6 us  [on_device(): pl.pallas_call(functools.partial(kernel, sizes), out_shape=(pltpu.VMEM(co...]
where the time goes in v6:
time: 23.6 us; the launch traced here: 23.5 us
  Pallas kernels  21.6 us (92%)
  local copies, waits for them, and re-layouts  1.28 us (5%)
  between operations  0.64 us (3%)
    pallas_call x1, Pallas kernels, on_device(): pl.pallas_call(functools.partial(kernel, sizes), out_shape=(pltpu.VMEM(co...  21.6 us
    unnamed x2, local copies, waits for them, and re-layouts  1.28 us

profile of v6, /device:TPU:0, one launch (start us, length us, event | category | flops | bytes accessed | tf_op | source)
XLA Modules:
  0.0 23.5 jit_solution(4288527329343873745)
XLA Ops:
  0.6 21.6 %shard_map.41 = (f32[5,8,8,128]{3,2,1,0:T(8,128)S(1)}, f32[8,8,128]{2,1,0:T(8,128)S(1)}) custom-call(f32[5,8,8,128]{3,2,1,0:T(8,128)} %cons_hbm.1, f32[8,8,128]{2,1,0:T(8,128)} %sig_hbm.1), custom_call_target="tpu_custom_call" | custom-call | tf_op jit(solution)/shard_map/pallas_call | solution.py:368
  22.2 0.7 %copy.6 = f32[5,8,8,128]{3,2,1,0:T(8,128)} copy(f32[5,8,8,128]{3,2,1,0:T(8,128)S(1)} %get-tuple-element.2) | data formatting | bytes 327680
  22.9 0.6 %copy.7 = f32[8,8,128]{2,1,0:T(8,128)} copy(f32[8,8,128]{2,1,0:T(8,128)S(1)} %get-tuple-element.3) | data formatting | bytes 65536
